TPU v7x, 32 devices: a whole 2x2x4 slice. The times are simulated.
32 devices in a mesh: dp: 2 (over x), ep: 16 (over z, y, core).
Axes of the slice: x: 2, y: 2, z: 4, core: 2. Of those that a mesh axis runs over, the one named last changes fastest.
Arguments:
- tok_rows: bfloat16 [16384, 2048], P(('dp', 'ep')), parts along dimension 0
- router_w: bfloat16 [2048, 64], replicated
- top_idx: int32 [16384, 6], P(('dp', 'ep')), parts along dimension 0
- slot_idx: int32 [16384, 6], P(('dp', 'ep')), parts along dimension 0
- w_gate: bfloat16 [80, 2048, 1408], P('ep')
- w_up: bfloat16 [80, 2048, 1408], P('ep')
- w_down: bfloat16 [80, 1408, 2048], P('ep')
- sh_gate: bfloat16 [2048, 2816], replicated
- sh_up: bfloat16 [2048, 2816], replicated
- sh_down: bfloat16 [2816, 2048], replicated
Outputs:
- output: bfloat16 [16384, 2048], P(('dp', 'ep')), parts along dimension 0
There are 2 independent parts. A program takes and returns all parts, laid end to end along the dimension named above; an argument that names none is the same for every part.
All inputs are finite; a program needn't handle non-finite values.
Results may differ from a plain program's by a relative error of at most 0.00103.
Values are sent between devices in bfloat16 or wider.
A program may use at most 1 GiB of HBM per device.

v0:
```python
import jax
import jax.numpy as jnp
from jax import lax
from jax.sharding import PartitionSpec as P

ROUTE_SCALE = 2.5


def solution(mesh):
    ep_size = mesh.shape['ep']

    def local_block(tok_rows, router_w, top_idx, slot_idx, w_gate, w_up, w_down, sh_gate, sh_up, sh_down):
        tok_count, hidden = tok_rows.shape
        top_k = top_idx.shape[1]
        dev_slots = w_gate.shape[0]
        num_slots = ep_size * dev_slots
        slot_cap = ((2 * tok_count * top_k + num_slots - 1) // num_slots + 7) // 8 * 8
        logits = jnp.dot(tok_rows, router_w, preferred_element_type=jnp.float32)
        picked = jax.nn.sigmoid(jnp.take_along_axis(logits, top_idx, axis=1))
        gate_wts = picked / jnp.sum(picked, axis=1, keepdims=True) * ROUTE_SCALE
        flat_slot = slot_idx.reshape(-1)
        slot_hot = (flat_slot[:, None] == jnp.arange(num_slots, dtype=jnp.int32)[None, :]).astype(jnp.int32)
        slot_rank = jnp.sum(jnp.cumsum(slot_hot, axis=0) * slot_hot, axis=1) - 1
        dest_row = flat_slot * slot_cap + slot_rank
        row_token = jnp.full((num_slots * slot_cap,), tok_count, jnp.int32).at[dest_row].set(jnp.arange(tok_count * top_k, dtype=jnp.int32) // top_k)
        send_rows = jnp.take(tok_rows, row_token, axis=0, mode='fill', fill_value=0).reshape(ep_size, dev_slots * slot_cap, hidden)
        recv_rows = lax.all_to_all(send_rows, 'ep', 0, 0, tiled=True).reshape(ep_size, dev_slots, slot_cap, hidden)
        gate_act = jnp.einsum('pskm,smf->spkf', recv_rows, w_gate, preferred_element_type=jnp.float32)
        up_act = jnp.einsum('pskm,smf->spkf', recv_rows, w_up, preferred_element_type=jnp.float32)
        hid_act = (jax.nn.silu(gate_act) * up_act).astype(jnp.bfloat16)
        exp_out = jnp.einsum('spkf,sfm->pskm', hid_act, w_down, preferred_element_type=jnp.float32).astype(jnp.bfloat16)
        back_rows = lax.all_to_all(exp_out.reshape(ep_size, dev_slots * slot_cap, hidden), 'ep', 0, 0, tiled=True)
        per_choice = jnp.take(back_rows.reshape(num_slots * slot_cap, hidden), dest_row, axis=0)
        routed = jnp.sum(per_choice.reshape(tok_count, top_k, hidden).astype(jnp.float32) * gate_wts[:, :, None], axis=1)
        sh_hid = (jax.nn.silu(jnp.dot(tok_rows, sh_gate, preferred_element_type=jnp.float32)) * jnp.dot(tok_rows, sh_up, preferred_element_type=jnp.float32)).astype(jnp.bfloat16)
        shared_out = jnp.dot(sh_hid, sh_down, preferred_element_type=jnp.float32)
        return (shared_out + routed).astype(jnp.bfloat16)

    tok_spec = P(('dp', 'ep'), None)
    slot_spec = P('ep', None, None)
    return jax.shard_map(local_block, mesh=mesh,
                         in_specs=(tok_spec, P(None, None), tok_spec, tok_spec, slot_spec, slot_spec, slot_spec,
                                   P(None, None), P(None, None), P(None, None)),
                         out_specs=tok_spec, check_vma=False)
```

profile of v0, /device:TPU:15, one launch (start us, length us, event | category | flops | bytes accessed | tf_op | source)
XLA Modules:
  0.0 1517.4 jit_solution(129026279150077856)
XLA Ops:
  0.0 1.0 copy.25
  1.0 0.2 eq.26
  1.4 0.7 broadcast_multiply_fusion
  2.1 1.0 fusion.11
  3.1 39.8 %reduce-window.6 = s32[80,24,128]{2,1,0:T(8,128)S(1)} reduce-window(s32[80,24,128]{2,1,0:T(8,128)} %fusion.11, s32[]{:T(128)} %constant.46.clone.1), window={size=1x1x128 pad=0_0x0_0x127_0}, to_apply=%region_0.0 | reduce-window | flops 31211520 | bytes 1966084 | tf_op jit(solution)/shard_map/reduce-window
  42.9 1.3 slice.14
  44.2 1.7 copy.41
  45.9 0.2 reduce-window.9
  46.1 0.3 broadcast_add_fusion
  46.4 0.2 fusion.10
  46.8 0.2 mul.57
  47.1 11.8 scatter_custom_fusion
  59.0 24.8 %gather_fusion = bf16[6400,2048]{1,0:T(8,128)(2,1)} fusion(bf16[512,2048]{1,0:T(8,128)(2,1)S(1)} %copy-done, s32[7168]{0:T(1024)S(1)} %pad_clamp_fusion), kind=kCustom, calls=%fused_computation | custom fusion | bytes 52454400 | tf_op jit(solution)/shard_map/jit(_take)/gather | solution.py:26
  83.8 18.0 %broadcast_select_fusion = bf16[16,400,2048]{2,1,0:T(8,128)(2,1)} fusion(bf16[16,400,2048]{2,1,0:T(8,128)(2,1)} %bitcast.53, pred[16,400]{1,0:T(8,128)(4,1)S(1)} %broadcast_in_dim.37), kind=kLoop, calls=%fused_computation.12 | loop fusion | flops 13107200 | bytes 52435200 | tf_op jit(solution)/shard_map/jit(_take)/select_n | solution.py:26
  101.8 572.2 %all_to_all.10 = bf16[16,400,2048]{2,1,0:T(8,128)(2,1)} all-to-all(bf16[16,400,2048]{2,1,0:T(8,128)(2,1)} %broadcast_select_fusion), channel_id=1, replica_groups=mesh['dp'=2,'ep'=16] {'ep'}, dimensions={0} | all-to-all | bytes 52428800 | tf_op jit(solution)/shard_map/all_to_all | solution.py:27
  674.0 48.8 %fusion.2 = f32[5,16,80,1408]{3,2,1,0:T(8,128)} fusion(bf16[5,2048,1408]{2,1,0:T(8,128)(2,1)} %param.15, bf16[16,5,80,2048]{3,2,1,0:T(8,128)(2,1)} %bitcast.55), kind=kOutput, calls=%fused_computation.8 | convolution fusion | flops 36909875200 | bytes 91095040 | tf_op jit(solution)/shard_map/pskm,smf->spkf/dot_general | solution.py:29
  722.8 53.1 %multiply_convert_fusion = bf16[5,16,80,1408]{3,2,1,0:T(8,128)(2,1)} fusion(f32[5,16,80,1408]{3,2,1,0:T(8,128)} %fusion.2, bf16[5,2048,1408]{2,1,0:T(8,128)(2,1)} %param.14, bf16[16,5,80,2048]{3,2,1,0:T(8,128)(2,1)} %bitcast.56), kind=kOutput, calls=%fused_computation.4 | convolution fusion | flops 36963942400 | bytes 109117440 | tf_op jit(solution)/shard_map/pskm,smf->spkf/dot_general | solution.py:28
  775.9 51.3 %convert_bitcast_fusion = bf16[16,5,80,2048]{3,2,0,1:T(8,128)(2,1)} fusion(bf16[5,16,80,1408]{3,2,1,0:T(8,128)(2,1)} %multiply_convert_fusion, bf16[5,1408,2048]{2,1,0:T(8,128)(2,1)} %param.16), kind=kOutput, calls=%fused_computation.11 | convolution fusion | flops 36922982400 | bytes 73072640 | tf_op jit(solution)/shard_map/spkf,sfm->pskm/dot_general | solution.py:31
  827.2 18.0 %copy.34 = bf16[16,5,80,2048]{3,2,1,0:T(8,128)(2,1)} copy(bf16[16,5,80,2048]{3,2,0,1:T(8,128)(2,1)} %convert_bitcast_fusion) | data formatting | bytes 52428800 | tf_op jit(solution)/shard_map/convert_element_type | solution.py:31
  845.2 5.7 all-to-all-start.1
  850.8 0.2 sub.15
  851.2 0.2 copy.30
  851.6 0.2 reshape.137
  851.8 0.8 fusion.19
  852.5 24.9 %gather_fusion.2 = f32[3072]{0:T(1024)S(1)} fusion(f32[512,64]{0,1:T(8,128)S(1)} %fusion.19, s32[3072]{0:T(1024)S(1)} %reshape.137), kind=kCustom, calls=%fused_computation.2 | custom fusion | bytes 49152 | tf_op jit(solution)/shard_map/jit(take_along_axis)/gather | solution.py:19
  877.4 0.2 reshape.140
  878.0 11.1 fusion.18
  889.1 526.7 %all-to-all-done.1 = bf16[16,400,2048]{2,1,0:T(8,128)(2,1)} async-done(((bf16[16,400,2048]{2,1,0:T(8,128)(2,1)}), bf16[16,400,2048]{2,1,0:T(8,128)(2,1)}, u32[]{:S(2)}, u32[]{:S(2)}) %all-to-all-start.1) | async-done | bytes 26214432 | tf_op jit(solution)/shard_map/all_to_all | solution.py:32
  1415.8 35.7 %gather_fusion.1 = bf16[3072,2048]{1,0:T(8,128)(2,1)} fusion(bf16[6400,2048]{1,0:T(8,128)(2,1)} %bitcast.15, s32[3072]{0:T(1024)S(1)} %broadcast_clamp_fusion), kind=kCustom, calls=%fused_computation.1 | custom fusion | bytes 25178112 | tf_op jit(solution)/shard_map/jit(_take)/gather | solution.py:33
  1451.5 20.4 %gather.19 = bf16[512,6,2048]{2,1,0:T(8,128)(2,1)} reshape(bf16[3072,2048]{1,0:T(8,128)(2,1)} %gather_fusion.1) | data formatting | bytes 25165824 | tf_op jit(solution)/shard_map/jit(_take)/gather | solution.py:33
  1471.8 21.2 %multiply_reduce_fusion = f32[512,2048]{1,0:T(8,128)} fusion(f32[512,6]{1,0:T(8,128)S(1)} %copy.37, bf16[512,6,2048]{2,1,0:T(8,128)(2,1)} %gather.19, pred[512,6]{1,0:T(8,128)(4,1)S(1)} %copy.30), kind=kLoop, calls=%fused_computation.5 | loop fusion | flops 24117248 | bytes 16792576 | tf_op jit(solution)/shard_map/reduce_sum | solution.py:34
  1493.1 23.9 %add_convert_fusion = bf16[512,2048]{1,0:T(8,128)(2,1)} fusion(f32[512,2048]{1,0:T(8,128)} %multiply_reduce_fusion, bf16[2816,2048]{1,0:T(8,128)(2,1)} %param.19, f32[512,2816]{1,0:T(8,128)} %fusion.18, bf16[512,2048]{1,0:T(8,128)(2,1)S(1)} %copy-done, bf16[2048,2816]{1,0:T(8,128)(2,1)} %param.18), kind=kOutput, calls=%fused_computation.16 | convolution fusion | flops 11821907968 | bytes 37224448 | tf_op jit(solution)/shard_map/dot_general | solution.py:36
  (34 shorter events, 1.1 us)
Async XLA Ops:
  0.0 59.0 %copy-start = (bf16[512,2048]{1,0:T(8,128)(2,1)S(1)}, bf16[512,2048]{1,0:T(8,128)(2,1)}, u32[]{:S(2)}) copy-start(bf16[512,2048]{1,0:T(8,128)(2,1)} %param.10) | copy-start | bytes 6291460
  46.7 37.1 %copy-start.4 = (s32[3072]{0:T(1024)}, s32[3072]{0:T(1024)S(1)}, u32[]{:S(2)}) copy-start(s32[3072]{0:T(1024)S(1)} %broadcast_add_fusion.1) | copy-start | bytes 36868
  47.1 36.8 %copy-start.6 = (s32[3072,1]{0,1:T(1,128)}, s32[3072,1]{0,1:T(1,128)S(1)}, u32[]{:S(2)}) copy-start(s32[3072,1]{0,1:T(1,128)S(1)} %compare_select_fusion.1) | copy-start | bytes 36868
  845.1 5.7 copy-start.5
  845.1 6.0 copy-start.2
  845.1 6.2 copy-start.3
  845.2 6.6 copy-start.1
  845.2 570.6 %all-to-all-start.1 = ((bf16[16,400,2048]{2,1,0:T(8,128)(2,1)}), bf16[16,400,2048]{2,1,0:T(8,128)(2,1)}, u32[]{:S(2)}, u32[]{:S(2)}) async-start(bf16[16,400,2048]{2,1,0:T(8,128)(2,1)} %bitcast.54), calls=%async_computation.1 | async-start | bytes 52428800 | tf_op jit(solution)/shard_map/all_to_all | solution.py:32
  852.5 25.5 %copy-start.7 = (s32[3072,1]{0,1:T(1,128)S(1)}, s32[3072,1]{0,1:T(1,128)}, u32[]{:S(2)}) copy-start(s32[3072,1]{0,1:T(1,128)} %copy-done.6) | copy-start | bytes 36868
where the time goes:
time: 1520 us
  blocking collectives  572 us (38%)
  waiting for transfers between devices  527 us (35%)
  matrix products  189 us (12%)
  local copies, waits for them, and re-layouts  142 us (9%)
  other arithmetic  81.6 us (5%)
    all_to_all x1, blocking collectives, local_block(): lax.all_to_all(send_rows, 'ep', 0, 0, tiled=True)  572 us
    all_to_all x1, waiting for transfers between devices, local_block(): lax.all_to_all(exp_out.reshape(ep_size, dev_slots * slot_cap, hidden), 'e...  527 us
    gather x2, local copies, waits for them, and re-layouts, local_block(): jnp.take(back_rows.reshape(num_slots * slot_cap, hidden), dest_row, axis=0)  56 us
    dot_general x1, matrix products, local_block(): jnp.einsum('pskm,smf->spkf', recv_rows, w_gate, preferred_element_type=jn...  53.1 us
    dot_general x1, matrix products, local_block(): jnp.einsum('spkf,sfm->pskm', hid_act, w_down, preferred_element_type=jnp....  51.3 us
    dot_general x1, matrix products, local_block(): jnp.einsum('pskm,smf->spkf', recv_rows, w_up, preferred_element_type=jnp....  48.8 us
    another operation x3, other arithmetic  40.4 us
  transfers between devices with their start and end apart: 1, of which 1 were waited for; matrix products, arithmetic and copies ran while one was open for 3% of the time, Pallas kernels for 0%

commit v1 on v0

v1 whole, which is shorter than its diff:
```python
import jax
import jax.numpy as jnp
from jax import lax
from jax.sharding import PartitionSpec as P

ROUTE_SCALE = 2.5


def solution(mesh):
    ep_size = mesh.shape['ep']

    def local_block(tok_rows, router_w, top_idx, slot_idx, w_gate, w_up, w_down, sh_gate, sh_up, sh_down):
        tok_count, hidden = tok_rows.shape
        top_k = top_idx.shape[1]
        dev_slots = w_gate.shape[0]
        num_slots = ep_size * dev_slots
        slot_cap = ((2 * tok_count * top_k + num_slots - 1) // num_slots + 7) // 8 * 8
        pair_rows = dev_slots * slot_cap
        me = lax.axis_index('ep')
        logits = jnp.dot(tok_rows, router_w, preferred_element_type=jnp.float32)
        scores = jax.nn.sigmoid(logits)
        exp_ids = jnp.arange(router_w.shape[1], dtype=jnp.int32)
        picked = jnp.sum(jnp.where(top_idx[:, :, None] == exp_ids, scores[:, None, :], 0.0), axis=2)
        gate_wts = picked / jnp.sum(picked, axis=1, keepdims=True) * ROUTE_SCALE
        meta = jnp.concatenate([slot_idx.astype(jnp.float32), gate_wts], axis=1)
        all_meta = lax.all_gather(meta, 'ep', axis=0, tiled=True)
        all_rows = lax.all_gather(tok_rows, 'ep', axis=0, tiled=False)

        sh_hid = (jax.nn.silu(jnp.dot(tok_rows, sh_gate, preferred_element_type=jnp.float32)) * jnp.dot(tok_rows, sh_up, preferred_element_type=jnp.float32)).astype(jnp.bfloat16)
        shared_out = jnp.dot(sh_hid, sh_down, preferred_element_type=jnp.float32)

        all_slot = all_meta[:, :top_k].astype(jnp.int32) - me * dev_slots
        all_gate = all_meta[:, top_k:]
        local_ids = jnp.arange(dev_slots, dtype=jnp.int32)
        match = all_slot[:, :, None] == local_ids
        hot = jnp.any(match, axis=1).reshape(ep_size, tok_count, dev_slots)
        gate_of = jnp.sum(jnp.where(match, all_gate[:, :, None], 0.0), axis=1).reshape(ep_size, tok_count, dev_slots)
        before = (jnp.arange(tok_count)[:, None] > jnp.arange(tok_count)[None, :]).astype(jnp.bfloat16)
        rank = jnp.einsum('mn,pns->pms', before, hot.astype(jnp.bfloat16), preferred_element_type=jnp.float32).astype(jnp.int32)
        row_of = jnp.where(hot, rank + local_ids * slot_cap, -1)
        row_ids = jnp.arange(pair_rows, dtype=jnp.int32)
        pick = sum((row_of[:, None, :, s] == row_ids[None, :, None]).astype(jnp.bfloat16) for s in range(dev_slots))
        slot_rows = jnp.einsum('pkn,pnm->pkm', pick, all_rows, preferred_element_type=jnp.float32).astype(jnp.bfloat16)
        recv_rows = slot_rows.reshape(ep_size, dev_slots, slot_cap, hidden)
        gate_act = jnp.einsum('pskm,smf->spkf', recv_rows, w_gate, preferred_element_type=jnp.float32)
        up_act = jnp.einsum('pskm,smf->spkf', recv_rows, w_up, preferred_element_type=jnp.float32)
        hid_act = (jax.nn.silu(gate_act) * up_act).astype(jnp.bfloat16)
        exp_out = jnp.einsum('spkf,sfm->pskm', hid_act, w_down, preferred_element_type=jnp.float32).astype(jnp.bfloat16)
        exp_out = exp_out.reshape(ep_size, pair_rows, hidden)
        weigh = sum(jnp.where(row_of[:, :, s, None] == row_ids, gate_of[:, :, s, None], 0.0) for s in range(dev_slots))
        hi = lax.reduce_precision(weigh, 8, 7)
        mid = lax.reduce_precision(weigh - hi, 8, 7)
        low = weigh - hi - mid
        partial = sum(jnp.einsum('pnk,pkm->pnm', part.astype(jnp.bfloat16), exp_out, preferred_element_type=jnp.float32) for part in (low, mid, hi))
        routed = lax.psum_scatter(partial.reshape(ep_size * tok_count, hidden), 'ep', scatter_dimension=0, tiled=True)
        return (shared_out + routed).astype(jnp.bfloat16)

    tok_spec = P(('dp', 'ep'), None)
    slot_spec = P('ep', None, None)
    return jax.shard_map(local_block, mesh=mesh,
                         in_specs=(tok_spec, P(None, None), tok_spec, tok_spec, slot_spec, slot_spec, slot_spec,
                                   P(None, None), P(None, None), P(None, None)),
                         out_specs=tok_spec, check_vma=False)
```

time: 1520 us -> 1200 us (0.79)
  the two profiles are of different devices: /device:TPU:15 before, /device:TPU:0 now
where the time goes in v1:
time: 1200 us; the launch traced here: 1190 us
  waiting for transfers between devices  757 us (63%)
  matrix products  371 us (31%)
  blocking collectives  27.6 us (2%)
  local copies, waits for them, and re-layouts  20.6 us (2%)
  between operations  14.1 us (1%)
    reduce_scatter x1, waiting for transfers between devices, local_block(): lax.psum_scatter(partial.reshape(ep_size * tok_count, hidden), 'ep', scat...  614 us
    dot_general x3, matrix products, local_block(): jnp.einsum('pnk,pkm->pnm', part.astype(jnp.bfloat16), exp_out, preferred_...  145 us
    all_gather x1, waiting for transfers between devices, local_block(): all_rows = lax.all_gather(tok_rows, 'ep', axis=0, tiled=False)  142 us
    dot_general x1, matrix products, local_block(): jnp.einsum('pskm,smf->spkf', recv_rows, w_gate, preferred_element_type=jn...  53.6 us
    dot_general x1, matrix products, local_block(): jnp.einsum('spkf,sfm->pskm', hid_act, w_down, preferred_element_type=jnp....  51.1 us
    dot_general x1, matrix products, local_block(): jnp.einsum('pskm,smf->spkf', recv_rows, w_up, preferred_element_type=jnp....  48.8 us
    dot_general x1, matrix products, local_block(): jnp.einsum('pkn,pnm->pkm', pick, all_rows, preferred_element_type=jnp.flo...  35.1 us
    all_gather x1, blocking collectives, local_block(): all_meta = lax.all_gather(meta, 'ep', axis=0, tiled=True)  27.6 us
  transfers between devices with their start and end apart: 2, of which 2 were waited for; matrix products, arithmetic and copies ran while one was open for 1% of the time, Pallas kernels for 0%

profile of v1, /device:TPU:0, one launch (start us, length us, event | category | flops | bytes accessed | tf_op | source)
XLA Modules:
  0.0 1193.1 jit_solution(11847061579389418197)
XLA Ops:
  6.5 0.0 copy-start
  6.5 0.0 all-gather.3.cloned.1.call-start
  6.5 0.7 all-gather.3.cloned.1.call-update
  7.3 0.0 reduce-scatter.2.cloned.1.call-start
  7.3 0.7 convert_element_type.55
  8.0 0.0 copy-done
  8.0 2.4 fusion.38
  10.4 0.9 select_reduce_fusion.1
  11.3 27.6 %all_gather.9 = f32[8192,12]{0,1:T(8,128)S(1)} all-gather(f32[512,12]{0,1:T(8,128)S(1)} %pad_maximum_fusion), channel_id=1, replica_groups=mesh['dp'=2,'ep'=16] {'ep'}, dimensions={0}, use_global_device_ids=true | all-gather | bytes 417792 | tf_op jit(solution)/shard_map/all_gather | solution.py:26
  39.0 0.4 select_reduce_fusion
  39.5 0.1 copy.39
  39.6 0.5 fusion.32
  40.1 0.3 fusion.35
  40.4 0.0 copy-start.2
  40.4 0.0 copy-start.4
  40.4 0.7 slice_bitcast_fusion.8
  41.2 141.8 %all-gather.3.cloned.1.call-done = bf16[8192,2048]{1,0:T(8,128)(2,1)} async-done(((bf16[512,2048]{1,0:T(8,128)(2,1)}), bf16[8192,2048]{1,0:T(8,128)(2,1)}) %all-gather.3.cloned.1.call-update) | async-done | bytes 33554448 | tf_op jit(solution)/shard_map/all_gather | solution.py:27
  183.0 35.1 %convolution_convert_fusion = bf16[16,400,2048]{2,1,0:T(8,128)(2,1)} fusion(bf16[16,512,2048]{2,1,0:T(8,128)(2,1)} %bitcast.81, s32[16,512]{1,0:T(8,128)S(1)} %get-tuple-element.13, s32[16,512]{1,0:T(8,128)S(1)} %get-tuple-element.14, s32[16,512]{1,0:T(8,128)S(1)} %get-tuple-element.15, s32[16,512]{1,0:T(8,128)S(1)} %get-tuple-element.16, ...), kind=kOutput, calls=%fused_computation.10 | convolution fusion | flops 13500416000 | bytes 59932672 | tf_op jit(solution)/shard_map/pkn,pnm->pkm/dot_general | solution.py:43
  218.1 0.0 copy-done.4
  218.1 48.8 %fusion.2 = f32[5,16,80,1408]{3,2,1,0:T(8,128)} fusion(bf16[5,2048,1408]{2,1,0:T(8,128)(2,1)} %param.15, bf16[16,5,80,2048]{3,2,1,0:T(8,128)(2,1)} %bitcast.82), kind=kOutput, calls=%fused_computation.4 | convolution fusion | flops 36909875200 | bytes 91095040 | tf_op jit(solution)/shard_map/pskm,smf->spkf/dot_general | solution.py:46
  266.9 53.6 %multiply_convert_fusion = bf16[5,16,80,1408]{3,2,1,0:T(8,128)(2,1)} fusion(f32[5,16,80,1408]{3,2,1,0:T(8,128)} %fusion.2, bf16[5,2048,1408]{2,1,0:T(8,128)(2,1)} %param.14, bf16[16,5,80,2048]{3,2,1,0:T(8,128)(2,1)} %bitcast.83), kind=kOutput, calls=%fused_computation.1 | convolution fusion | flops 36963942400 | bytes 109117440 | tf_op jit(solution)/shard_map/pskm,smf->spkf/dot_general | solution.py:45
  320.5 51.1 %convert_bitcast_fusion = bf16[16,5,80,2048]{3,2,0,1:T(8,128)(2,1)} fusion(bf16[5,16,80,1408]{3,2,1,0:T(8,128)(2,1)} %multiply_convert_fusion, bf16[5,1408,2048]{2,1,0:T(8,128)(2,1)} %param.16), kind=kOutput, calls=%fused_computation.7 | convolution fusion | flops 36922982400 | bytes 73072640 | tf_op jit(solution)/shard_map/spkf,sfm->pskm/dot_general | solution.py:48
  371.7 0.0 copy-start.12
  371.7 18.1 %copy.24 = bf16[16,5,80,2048]{3,2,1,0:T(8,128)(2,1)} copy(bf16[16,5,80,2048]{3,2,0,1:T(8,128)(2,1)} %convert_bitcast_fusion) | data formatting | bytes 52428800 | tf_op jit(solution)/shard_map/convert_element_type | solution.py:48
  389.9 35.2 %fusion.26 = f32[16,512,2048]{2,1,0:T(8,128)} fusion(bf16[16,400,2048]{2,1,0:T(8,128)(2,1)} %bitcast.75, f32[16,512]{1,0:T(8,128)S(1)} %copy-done.13, s32[16,512]{1,0:T(8,128)S(1)} %copy-done.5, f32[16,512]{1,0:T(8,128)S(1)} %copy-done.14, s32[16,512]{1,0:T(8,128)S(1)} %copy-done.7, f32[16,512]{1,0:T(8,128)S(1)} %copy-done.15, s32[16,512]{1,0:T(8,128)S(1)} %copy-done.9, ...), kind=kOutput, calls=%fused_computation.37 | convolution fusion | flops 13480755200 | bytes 93650944 | tf_op jit(solution)/shard_map/pnk,pkm->pnm/dot_general | solution.py:54
  425.2 35.3 %fusion.24 = f32[16,512,2048]{2,1,0:T(8,128)} fusion(bf16[16,400,2048]{2,1,0:T(8,128)(2,1)} %bitcast.76, f32[16,512]{1,0:T(8,128)S(1)} %copy-done.13, s32[16,512]{1,0:T(8,128)S(1)} %copy-done.5, f32[16,512]{1,0:T(8,128)S(1)} %copy-done.14, s32[16,512]{1,0:T(8,128)S(1)} %copy-done.7, f32[16,512]{1,0:T(8,128)S(1)} %copy-done.15, s32[16,512]{1,0:T(8,128)S(1)} %copy-done.9, ...), kind=kOutput, calls=%fused_computation.36 | convolution fusion | flops 13484032000 | bytes 93650944 | tf_op jit(solution)/shard_map/pnk,pkm->pnm/dot_general | solution.py:54
  460.4 74.5 %add_add_fusion = f32[16,512,2048]{2,1,0:T(8,128)} fusion(f32[16,512,2048]{2,1,0:T(8,128)} %fusion.24, f32[16,512,2048]{2,1,0:T(8,128)} %fusion.26, bf16[16,400,2048]{2,1,0:T(8,128)(2,1)} %bitcast.77, f32[16,512]{1,0:T(8,128)S(1)} %copy-done.13, s32[16,512]{1,0:T(8,128)S(1)} %copy-done.5, f32[16,512]{1,0:T(8,128)S(1)} %copy-done.14, ...), kind=kOutput, calls=%fused_computation | convolution fusion | flops 13507756032 | bytes 227868672 | tf_op jit(solution)/shard_map/pnk,pkm->pnm/dot_general | solution.py:54
  534.9 0.0 reduce-scatter.2.cloned.1.call-update
  535.0 1.6 copy-done.17
  536.5 11.1 fusion.48
  547.6 614.3 %reduce-scatter.2.cloned.1.call-done = f32[512,2048]{1,0:T(8,128)} async-done(((f32[8192,2048]{1,0:T(8,128)}), f32[512,2048]{1,0:T(8,128)}) %reduce-scatter.2.cloned.1.call-update) | async-done | bytes 4194320 | tf_op jit(solution)/shard_map/reduce_scatter | solution.py:55
  1161.9 24.0 %add_convert_fusion = bf16[512,2048]{1,0:T(8,128)(2,1)} fusion(f32[512,2048]{1,0:T(8,128)} %reduce-scatter.2.cloned.1.call-done, bf16[2816,2048]{1,0:T(8,128)(2,1)} %param.19, f32[512,2816]{1,0:T(8,128)} %fusion.48, bf16[512,2048]{1,0:T(8,128)(2,1)S(1)} %copy-done.17, bf16[2048,2816]{1,0:T(8,128)(2,1)} %param.18), kind=kOutput, calls=%fused_computation.44 | convolution fusion | flops 11821907968 | bytes 37224448 | tf_op jit(solution)/shard_map/dot_general | solution.py:30
  (35 shorter events, 0.2 us)
Async XLA Ops:
  6.5 1.5 copy-start
  6.5 176.5 %all-gather.3.cloned.1.call-start = ((), (), s32[]{:S(2)}) async-start(), calls=%async_computation.2 | async-start | bytes 35651584 | tf_op jit(solution)/shard_map/all_gather | solution.py:27
  7.3 1154.7 %reduce-scatter.2.cloned.1.call-start = ((), (), s32[]{:S(2)}) async-start(), calls=%async_computation.1 | async-start | bytes 71303168 | tf_op jit(solution)/shard_map/reduce_scatter | solution.py:55
  40.4 177.7 %copy-start.2 = (s32[16,512]{1,0:T(8,128)}, s32[16,512]{1,0:T(8,128)S(1)}, u32[]{:S(2)}) copy-start(s32[16,512]{1,0:T(8,128)S(1)} %get-tuple-element.12) | copy-start | bytes 98308
  40.4 177.7 %copy-start.4 = (s32[16,512]{1,0:T(8,128)}, s32[16,512]{1,0:T(8,128)S(1)}, u32[]{:S(2)}) copy-start(s32[16,512]{1,0:T(8,128)S(1)} %get-tuple-element.13) | copy-start | bytes 98308
  40.4 177.7 %copy-start.6 = (s32[16,512]{1,0:T(8,128)}, s32[16,512]{1,0:T(8,128)S(1)}, u32[]{:S(2)}) copy-start(s32[16,512]{1,0:T(8,128)S(1)} %get-tuple-element.14) | copy-start | bytes 98308
  40.4 177.7 %copy-start.8 = (s32[16,512]{1,0:T(8,128)}, s32[16,512]{1,0:T(8,128)S(1)}, u32[]{:S(2)}) copy-start(s32[16,512]{1,0:T(8,128)S(1)} %get-tuple-element.15) | copy-start | bytes 98308
  40.4 177.7 %copy-start.10 = (s32[16,512]{1,0:T(8,128)}, s32[16,512]{1,0:T(8,128)S(1)}, u32[]{:S(2)}) copy-start(s32[16,512]{1,0:T(8,128)S(1)} %get-tuple-element.16) | copy-start | bytes 98308
  371.6 18.2 %copy-start.3 = (s32[16,512]{1,0:T(8,128)S(1)}, s32[16,512]{1,0:T(8,128)}, u32[]{:S(2)}) copy-start(s32[16,512]{1,0:T(8,128)} %copy-done.2) | copy-start | bytes 98308
  371.6 18.2 %copy-start.5 = (s32[16,512]{1,0:T(8,128)S(1)}, s32[16,512]{1,0:T(8,128)}, u32[]{:S(2)}) copy-start(s32[16,512]{1,0:T(8,128)} %copy-done.4) | copy-start | bytes 98308
  371.6 18.2 %copy-start.7 = (s32[16,512]{1,0:T(8,128)S(1)}, s32[16,512]{1,0:T(8,128)}, u32[]{:S(2)}) copy-start(s32[16,512]{1,0:T(8,128)} %copy-done.6) | copy-start | bytes 98308
  371.7 18.2 %copy-start.9 = (s32[16,512]{1,0:T(8,128)S(1)}, s32[16,512]{1,0:T(8,128)}, u32[]{:S(2)}) copy-start(s32[16,512]{1,0:T(8,128)} %copy-done.8) | copy-start | bytes 98308
  371.7 18.2 %copy-start.11 = (s32[16,512]{1,0:T(8,128)S(1)}, s32[16,512]{1,0:T(8,128)}, u32[]{:S(2)}) copy-start(s32[16,512]{1,0:T(8,128)} %copy-done.10) | copy-start | bytes 98308
  371.7 18.2 %copy-start.12 = (f32[16,512]{1,0:T(8,128)S(1)}, f32[16,512]{1,0:T(8,128)}, u32[]{:S(2)}) copy-start(f32[16,512]{1,0:T(8,128)} %get-tuple-element.7) | copy-start | bytes 98308
  371.7 18.2 %copy-start.13 = (f32[16,512]{1,0:T(8,128)S(1)}, f32[16,512]{1,0:T(8,128)}, u32[]{:S(2)}) copy-start(f32[16,512]{1,0:T(8,128)} %get-tuple-element.8) | copy-start | bytes 98308
  371.7 18.2 %copy-start.14 = (f32[16,512]{1,0:T(8,128)S(1)}, f32[16,512]{1,0:T(8,128)}, u32[]{:S(2)}) copy-start(f32[16,512]{1,0:T(8,128)} %get-tuple-element.9) | copy-start | bytes 98308
  371.7 18.2 %copy-start.15 = (f32[16,512]{1,0:T(8,128)S(1)}, f32[16,512]{1,0:T(8,128)}, u32[]{:S(2)}) copy-start(f32[16,512]{1,0:T(8,128)} %get-tuple-element.10) | copy-start | bytes 98308
  371.7 18.2 %copy-start.16 = (f32[16,512]{1,0:T(8,128)S(1)}, f32[16,512]{1,0:T(8,128)}, u32[]{:S(2)}) copy-start(f32[16,512]{1,0:T(8,128)} %get-tuple-element.11) | copy-start | bytes 98308
  534.9 1.6 copy-start.17
  1161.9 24.0 %copy-start.1 = (bf16[2048,64]{0,1:T(8,128)(2,1)S(1)}, bf16[2048,64]{0,1:T(8,128)(2,1)}, u32[]{:S(2)}) copy-start(bf16[2048,64]{0,1:T(8,128)(2,1)} %param.11) | copy-start | bytes 786436
Sparse Core Ops, SparseCore 0:
  8.9 174.0 all-gather.2
  535.1 626.7 reduce-scatter.1

commit v2 on v1

--- a/solution.py
+++ b/solution.py
@@ -1,9 +1,166 @@
+import functools
+
 import jax
 import jax.numpy as jnp
 from jax import lax
+from jax.experimental import pallas as pl
+from jax.experimental.pallas import tpu as pltpu
 from jax.sharding import PartitionSpec as P
 
 ROUTE_SCALE = 2.5
+MESH = pl.DeviceIdType.MESH
+
+
+def ring_of(idx):
+    z, y, core = idx // 4, (idx // 2) % 2, idx % 2
+    return (z + y * (7 - 2 * z)) * 2 + core
+
+
+def index_of(pos):
+    pos = (pos + 32) % 16
+    chip, core = pos // 2, pos % 2
+    back = chip // 4
+    z = chip + back * (7 - 2 * chip)
+    return z * 4 + back * 2 + core
+
+
+def reduce_kernel(hid_hbm, weigh_hbm, down_hbm, out_hbm, down_v, hid_v, weigh_v, tri_v, own_v, run_v,
+                  down_sem, hid_sem, weigh_sem, send_sem, recv_sem, free_sem, out_sem):
+    steps = weigh_hbm.shape[0]
+    dev_slots, slot_cap, _ = hid_v.shape[2:]
+    pair_rows = dev_slots * slot_cap
+    half = run_v.shape[4]
+    sub_rows = run_v.shape[3]
+    col_tile = min(512, half)
+    mix_tile = min(256, half)
+    pos = ring_of(lax.axis_index('ep'))
+    ahead = (index_of(pos + 1), index_of(pos - 1))
+    behind = (index_of(pos - 1), index_of(pos + 1))
+
+    barrier = pltpu.get_barrier_semaphore()
+    for peer in ahead:
+        pl.semaphore_signal(barrier, inc=1, device_id={'ep': peer}, device_id_type=MESH)
+
+    def block_of(step, way):
+        return index_of(pos - 1 - step) if way == 0 else index_of(pos + 1 + step)
+
+    def fetches(step, way):
+        par = step % 2
+        block = block_of(step, way)
+        return (pltpu.make_async_copy(hid_hbm.at[:, block], hid_v.at[par, way], hid_sem.at[par, way]),
+                pltpu.make_async_copy(weigh_hbm.at[block], weigh_v.at[par, way], weigh_sem.at[par, way]))
+
+    def start_fetch(step):
+        for way in (0, 1):
+            for copy in fetches(step, way):
+                copy.start()
+
+    def compute_own(step):
+        par = step % 2
+        for way in (0, 1):
+            for copy in fetches(step, way):
+                copy.wait()
+
+            def one_slot(slot, _):
+                for col in range(0, half, col_tile):
+                    rows = jnp.dot(hid_v[par, way, slot], down_v[slot, :, way * half + col:way * half + col + col_tile],
+                                   preferred_element_type=jnp.float32).astype(jnp.bfloat16)
+                    for part in range(3):
+                        at = pl.multiple_of(slot * slot_cap + part * pair_rows, 16)
+                        tri_v[pl.ds(at, slot_cap), col:col + col_tile] = rows
+                return 0
+
+            lax.fori_loop(0, dev_slots, one_slot, 0)
+
+            def one_tile(tile, _):
+                cols = pl.ds(pl.multiple_of(tile * mix_tile, mix_tile), mix_tile)
+                own_v[way, :, cols] = jnp.dot(weigh_v[par, way], tri_v[:, cols], preferred_element_type=jnp.float32)
+                return 0
+
+            lax.fori_loop(0, half // mix_tile, one_tile, 0)
+
+    def send(step, way, sub):
+        now, later = step % 2, (step + 1) % 2
+        return pltpu.make_async_remote_copy(
+            src_ref=run_v.at[way, now, sub], dst_ref=run_v.at[way, later, sub],
+            send_sem=send_sem.at[way, now, sub], recv_sem=recv_sem.at[way, later, sub],
+            device_id={'ep': ahead[way]}, device_id_type=MESH)
+
+    down_copy = pltpu.make_async_copy(down_hbm, down_v, down_sem)
+    down_copy.start()
+    start_fetch(0)
+    start_fetch(1)
+    down_copy.wait()
+    compute_own(0)
+    start_fetch(2)
+    pl.semaphore_wait(barrier, 2)
+    for sub in (0, 1):
+        for way in (0, 1):
+            run_v[way, 0, sub] = own_v[way, sub * sub_rows:(sub + 1) * sub_rows, :]
+            send(0, way, sub).start()
+    compute_own(1)
+    start_fetch(3)
+
+    def one_step(step, _):
+        now = step % 2
+        for sub in (0, 1):
+            for way in (0, 1):
+                send(step - 1, way, sub).wait_recv()
+                send(step - 1, way, sub).wait_send()
+                pl.semaphore_signal(free_sem.at[way, sub], inc=1, device_id={'ep': behind[way]}, device_id_type=MESH)
+                run_v[way, now, sub] += own_v[way, sub * sub_rows:(sub + 1) * sub_rows, :]
+                pl.semaphore_wait(free_sem.at[way, sub], 1)
+                send(step, way, sub).start()
+        compute_own(step + 1)
+
+        @pl.when(step + 3 < steps)
+        def _():
+            start_fetch(step + 3)
+        return 0
+
+    lax.fori_loop(1, steps - 1, one_step, 0)
+    last = (steps - 1) % 2
+    outs = []
+    for sub in (0, 1):
+        for way in (0, 1):
+            send(steps - 2, way, sub).wait_recv()
+            send(steps - 2, way, sub).wait_send()
+            run_v[way, last, sub] += own_v[way, sub * sub_rows:(sub + 1) * sub_rows, :]
+            outs.append(pltpu.make_async_copy(run_v.at[way, last, sub],
+                                              out_hbm.at[pl.ds(sub * sub_rows, sub_rows), pl.ds(way * half, half)],
+                                              out_sem.at[way, sub]))
+            outs[-1].start()
+    for copy in outs:
+        copy.wait()
+
+
+def reduce_home(hid, weigh, w_down):
+    dev_slots, steps, slot_cap, ff = hid.shape
+    tok_count = weigh.shape[1]
+    hidden = w_down.shape[2]
+    half, sub_rows = hidden // 2, tok_count // 2
+    any_spec = pl.BlockSpec(memory_space=pl.ANY)
+    dma = pltpu.SemaphoreType.DMA
+    flops = 2 * steps * dev_slots * slot_cap * hidden * (ff + 3 * tok_count)
+    return pl.pallas_call(
+        reduce_kernel,
+        out_shape=jax.ShapeDtypeStruct((tok_count, hidden), jnp.float32),
+        in_specs=[any_spec] * 3,
+        out_specs=any_spec,
+        scratch_shapes=[
+            pltpu.VMEM((dev_slots, ff, hidden), jnp.bfloat16),
+            pltpu.VMEM((2, 2, dev_slots, slot_cap, ff), jnp.bfloat16),
+            pltpu.VMEM((2, 2, tok_count, weigh.shape[2]), jnp.bfloat16),
+            pltpu.VMEM((weigh.shape[2], half), jnp.bfloat16),
+            pltpu.VMEM((2, tok_count, half), jnp.float32),
+            pltpu.VMEM((2, 2, 2, sub_rows, half), jnp.float32),
+            dma, dma((2, 2)), dma((2, 2)), dma((2, 2, 2)), dma((2, 2, 2)),
+            pltpu.SemaphoreType.REGULAR((2, 2)), dma((2, 2)),
+        ],
+        compiler_params=pltpu.CompilerParams(collective_id=1, has_side_effects=True, vmem_limit_bytes=65_000_000),
+        cost_estimate=pl.CostEstimate(flops=flops, bytes_accessed=70_000_000, transcendentals=0),
+        name='reduce_home',
+    )(hid, weigh, w_down)
 
 
 def solution(mesh):
@@ -14,7 +171,7 @@
         top_k = top_idx.shape[1]
         dev_slots = w_gate.shape[0]
         num_slots = ep_size * dev_slots
-        slot_cap = ((2 * tok_count * top_k + num_slots - 1) // num_slots + 7) // 8 * 8
+        slot_cap = ((2 * tok_count * top_k + num_slots - 1) // num_slots + 15) // 16 * 16
         pair_rows = dev_slots * slot_cap
         me = lax.axis_index('ep')
         logits = jnp.dot(tok_rows, router_w, preferred_element_type=jnp.float32)
@@ -39,20 +196,18 @@
         rank = jnp.einsum('mn,pns->pms', before, hot.astype(jnp.bfloat16), preferred_element_type=jnp.float32).astype(jnp.int32)
         row_of = jnp.where(hot, rank + local_ids * slot_cap, -1)
         row_ids = jnp.arange(pair_rows, dtype=jnp.int32)
+        weigh = sum(jnp.where(row_of[:, :, s, None] == row_ids, gate_of[:, :, s, None], 0.0) for s in range(dev_slots))
+        hi = lax.reduce_precision(weigh, 8, 7)
+        mid = lax.reduce_precision(weigh - hi, 8, 7)
+        low = weigh - hi - mid
+        weigh3 = jnp.concatenate([low.astype(jnp.bfloat16), mid.astype(jnp.bfloat16), hi.astype(jnp.bfloat16)], axis=2)
         pick = sum((row_of[:, None, :, s] == row_ids[None, :, None]).astype(jnp.bfloat16) for s in range(dev_slots))
         slot_rows = jnp.einsum('pkn,pnm->pkm', pick, all_rows, preferred_element_type=jnp.float32).astype(jnp.bfloat16)
         recv_rows = slot_rows.reshape(ep_size, dev_slots, slot_cap, hidden)
         gate_act = jnp.einsum('pskm,smf->spkf', recv_rows, w_gate, preferred_element_type=jnp.float32)
         up_act = jnp.einsum('pskm,smf->spkf', recv_rows, w_up, preferred_element_type=jnp.float32)
         hid_act = (jax.nn.silu(gate_act) * up_act).astype(jnp.bfloat16)
-        exp_out = jnp.einsum('spkf,sfm->pskm', hid_act, w_down, preferred_element_type=jnp.float32).astype(jnp.bfloat16)
-        exp_out = exp_out.reshape(ep_size, pair_rows, hidden)
-        weigh = sum(jnp.where(row_of[:, :, s, None] == row_ids, gate_of[:, :, s, None], 0.0) for s in range(dev_slots))
-        hi = lax.reduce_precision(weigh, 8, 7)
-        mid = lax.reduce_precision(weigh - hi, 8, 7)
-        low = weigh - hi - mid
-        partial = sum(jnp.einsum('pnk,pkm->pnm', part.astype(jnp.bfloat16), exp_out, preferred_element_type=jnp.float32) for part in (low, mid, hi))
-        routed = lax.psum_scatter(partial.reshape(ep_size * tok_count, hidden), 'ep', scatter_dimension=0, tiled=True)
+        routed = reduce_home(hid_act, weigh3, w_down)
         return (shared_out + routed).astype(jnp.bfloat16)
 
     tok_spec = P(('dp', 'ep'), None)

time: 1200 us -> 715 us (0.60)
  waiting for transfers between devices: 757 us -> 81.3 us
  Pallas kernels: 0 us -> 363 us
  matrix products: 371 us -> 175 us
  other arithmetic: 2.57 us -> 18 us
  local copies, waits for them, and re-layouts: 20.6 us -> 35.7 us
    reduce_scatter x1 -> x0, waiting for transfers between devices: 614 us -> none  [local_block(): lax.psum_scatter(partial.reshape(ep_size * tok_count, hidden), 'ep', scat...]
    pallas_call x0 -> x1, Pallas kernels: none -> 363 us  [reduce_home(): pl.pallas_call(reduce_kernel, out_shape=jax.ShapeDtypeStruct((tok_count,...]
    dot_general x4 -> x0, matrix products: 196 us -> none  [the longest x3 145 us: local_block(): jnp.einsum('pnk,pkm->pnm', part.astype(jnp.bfloat16), exp_out, preferred_...]
    all_gather x1, waiting for transfers between devices: 142 us -> 80.6 us  [local_block(): all_rows = lax.all_gather(tok_rows, 'ep', axis=0, tiled=False)]
    concatenate x0 -> x1, local copies, waits for them, and re-layouts: none -> 35.5 us  [local_block(): jnp.concatenate([low.astype(jnp.bfloat16), mid.astype(jnp.bfloat16), hi.a...]
    convert_element_type x1 -> x0, local copies, waits for them, and re-layouts: 18.1 us -> none  [local_block(): jnp.einsum('spkf,sfm->pskm', hid_act, w_down, preferred_element_type=jnp....]
    convert_element_type x0 -> x1, other arithmetic: none -> 15.4 us  [local_block(): hi.astype(jnp.bfloat16)]
  transfers between devices with their start and end apart: 2 -> 1, of which waited for: 2 -> 1; matrix products, arithmetic and copies ran while one was open for 1% -> 9% of each run, Pallas kernels for 0% -> 0%
where the time goes in v2:
time: 715 us; the launch traced here: 714 us
  Pallas kernels  363 us (51%)
  matrix products  175 us (24%)
  waiting for transfers between devices  81.3 us (11%)
  local copies, waits for them, and re-layouts  35.7 us (5%)
  blocking collectives  27.6 us (4%)
  other arithmetic  18 us (3%)
  between operations  13.5 us (2%)
    pallas_call x1, Pallas kernels, reduce_home(): pl.pallas_call(reduce_kernel, out_shape=jax.ShapeDtypeStruct((tok_count,...  363 us
    all_gather x1, waiting for transfers between devices, local_block(): all_rows = lax.all_gather(tok_rows, 'ep', axis=0, tiled=False)  80.6 us
    dot_general x1, matrix products, local_block(): jnp.einsum('pskm,smf->spkf', recv_rows, w_gate, preferred_element_type=jn...  53.1 us
    dot_general x1, matrix products, local_block(): jnp.einsum('pskm,smf->spkf', recv_rows, w_up, preferred_element_type=jnp....  48.8 us
    concatenate x1, local copies, waits for them, and re-layouts, local_block(): jnp.concatenate([low.astype(jnp.bfloat16), mid.astype(jnp.bfloat16), hi.a...  35.5 us
    dot_general x1, matrix products, local_block(): jnp.einsum('pkn,pnm->pkm', pick, all_rows, preferred_element_type=jnp.flo...  35 us
    all_gather x1, blocking collectives, local_block(): all_meta = lax.all_gather(meta, 'ep', axis=0, tiled=True)  27.6 us
    dot_general x1, matrix products, local_block(): shared_out = jnp.dot(sh_hid, sh_down, preferred_element_type=jnp.float32)  24.5 us
  transfers between devices with their start and end apart: 1, of which 1 were waited for; matrix products, arithmetic and copies ran while one was open for 9% of the time, Pallas kernels for 0%

profile of v2, /device:TPU:0, one launch (start us, length us, event | category | flops | bytes accessed | tf_op | source)
XLA Modules:
  0.0 713.8 jit_solution(4754931806716771096)
XLA Ops:
  6.5 0.0 copy-start
  6.5 0.0 all-gather.3.cloned.1.call-start
  6.5 0.7 all-gather.3.cloned.1.call-update
  7.3 0.7 convert_element_type.49
  8.0 0.0 copy-done
  8.0 2.4 fusion.31
  10.4 0.9 select_reduce_fusion.1
  11.3 27.6 %all_gather.9 = f32[8192,12]{0,1:T(8,128)S(1)} all-gather(f32[512,12]{0,1:T(8,128)S(1)} %pad_maximum_fusion), channel_id=1, replica_groups=mesh['dp'=2,'ep'=16] {'ep'}, dimensions={0}, use_global_device_ids=true | all-gather | bytes 417792 | tf_op jit(solution)/shard_map/all_gather | solution.py:183
  39.0 0.4 select_reduce_fusion
  39.4 0.1 copy.32
  39.5 0.5 fusion.25
  40.0 0.3 fusion.28
  40.4 15.4 %reduce-precision_convert_fusion.1 = (bf16[16,512,400]{2,1,0:T(8,128)(2,1)}, bf16[16,512,400]{2,1,0:T(8,128)(2,1)}, bf16[16,512,400]{2,1,0:T(8,128)(2,1)}) fusion(f32[16,512]{1,0:T(8,128)S(1)} %get-tuple-element.11, s32[16,512]{1,0:T(8,128)S(1)} %get-tuple-element.16, f32[16,512]{1,0:T(8,128)S(1)} %get-tuple-element.12, s32[16,512]{1,0:T(8,128)S(1)} %get-tuple-element.17, ...), kind=kLoop, calls=%fused_computation.6 | loop fusion | flops 68812800 | bytes 19988480 | tf_op jit(solution)/shard_map/convert_element_type | solution.py:203
  55.8 0.0 copy-start.2
  55.8 35.5 %concatenate.7.weigh_hbm = bf16[16,512,1200]{2,1,0:T(8,128)(2,1)} concatenate(bf16[16,512,400]{2,1,0:T(8,128)(2,1)} %get-tuple-element.9, bf16[16,512,400]{2,1,0:T(8,128)(2,1)} %get-tuple-element.8, bf16[16,512,400]{2,1,0:T(8,128)(2,1)} %get-tuple-element.7), dimensions={2} | concatenate | bytes 39321600 | tf_op jit(solution)/shard_map/concatenate | solution.py:203
  91.3 0.0 copy-done.2
  91.3 11.1 %fusion.38 = f32[512,2816]{1,0:T(8,128)} fusion(bf16[512,2048]{1,0:T(8,128)(2,1)S(1)} %copy-done.2, bf16[2048,2816]{1,0:T(8,128)(2,1)} %param.17), kind=kOutput, calls=%fused_computation.74 | convolution fusion | flops 5905580032 | bytes 19398656 | tf_op jit(solution)/shard_map/dot_general | solution.py:186
  102.4 80.6 %all-gather.3.cloned.1.call-done = bf16[8192,2048]{1,0:T(8,128)(2,1)} async-done(((bf16[512,2048]{1,0:T(8,128)(2,1)}), bf16[8192,2048]{1,0:T(8,128)(2,1)}) %all-gather.3.cloned.1.call-update) | async-done | bytes 33554448 | tf_op jit(solution)/shard_map/all_gather | solution.py:184
  182.9 35.0 %convolution_convert_fusion = bf16[16,400,2048]{2,1,0:T(8,128)(2,1)} fusion(bf16[16,512,2048]{2,1,0:T(8,128)(2,1)} %bitcast.62, s32[16,512]{1,0:T(8,128)S(1)} %get-tuple-element.16, s32[16,512]{1,0:T(8,128)S(1)} %get-tuple-element.17, s32[16,512]{1,0:T(8,128)S(1)} %get-tuple-element.18, s32[16,512]{1,0:T(8,128)S(1)} %get-tuple-element.19, ...), kind=kOutput, calls=%fused_computation.10 | convolution fusion | flops 13500416000 | bytes 59932672 | tf_op jit(solution)/shard_map/pkn,pnm->pkm/dot_general | solution.py:205
  218.0 48.8 %fusion = f32[5,16,80,1408]{3,2,1,0:T(8,128)} fusion(bf16[5,2048,1408]{2,1,0:T(8,128)(2,1)} %param.15, bf16[16,5,80,2048]{3,2,1,0:T(8,128)(2,1)} %bitcast.63), kind=kOutput, calls=%fused_computation.1 | convolution fusion | flops 36909875200 | bytes 91095040 | tf_op jit(solution)/shard_map/pskm,smf->spkf/dot_general | solution.py:208
  266.8 53.1 %multiply_convert_fusion.hid_hbm = bf16[5,16,80,1408]{3,2,1,0:T(8,128)(2,1)} fusion(f32[5,16,80,1408]{3,2,1,0:T(8,128)} %fusion, bf16[5,2048,1408]{2,1,0:T(8,128)(2,1)} %param.14, bf16[16,5,80,2048]{3,2,1,0:T(8,128)(2,1)} %bitcast.64), kind=kOutput, calls=%fused_computation | convolution fusion | flops 36963942400 | bytes 109117440 | tf_op jit(solution)/shard_map/pskm,smf->spkf/dot_general | solution.py:207
  319.9 362.5 %reduce_home.1 = f32[512,2048]{1,0:T(8,128)} custom-call(bf16[5,16,80,1408]{3,2,1,0:T(8,128)(2,1)} %multiply_convert_fusion.hid_hbm, bf16[16,512,1200]{2,1,0:T(8,128)(2,1)} %concatenate.7.weigh_hbm, bf16[5,1408,2048]{2,1,0:T(8,128)(2,1)} %down_hbm.1), custom_call_target="tpu_custom_call" | custom-call | flops 77175193600 | bytes 70000000 | tf_op jit(solution)/shard_map/reduce_home/pallas_call | solution.py:145
  682.4 0.0 copy-start.1
  682.4 24.5 %add_convert_fusion = bf16[512,2048]{1,0:T(8,128)(2,1)} fusion(f32[512,2048]{1,0:T(8,128)} %reduce_home.1, bf16[2816,2048]{1,0:T(8,128)(2,1)} %param.19, f32[512,2816]{1,0:T(8,128)} %fusion.38, bf16[512,2048]{1,0:T(8,128)(2,1)} %param.10, bf16[2048,2816]{1,0:T(8,128)(2,1)} %param.18), kind=kOutput, calls=%fused_computation.38 | convolution fusion | flops 11821907968 | bytes 37224448 | tf_op jit(solution)/shard_map/dot_general | solution.py:187
  707.0 0.0 copy-done.1
  (7 shorter events, 0.1 us)
Async XLA Ops:
  6.5 1.5 copy-start
  6.5 176.4 %all-gather.3.cloned.1.call-start = ((), (), s32[]{:S(2)}) async-start(), calls=%async_computation | async-start | bytes 35651584 | tf_op jit(solution)/shard_map/all_gather | solution.py:184
  55.8 35.5 %copy-start.2 = (bf16[512,2048]{1,0:T(8,128)(2,1)S(1)}, bf16[512,2048]{1,0:T(8,128)(2,1)}, u32[]{:S(2)}) copy-start(bf16[512,2048]{1,0:T(8,128)(2,1)} %param.10) | copy-start | bytes 6291460
  682.4 24.6 %copy-start.1 = (bf16[2048,64]{0,1:T(8,128)(2,1)S(1)}, bf16[2048,64]{0,1:T(8,128)(2,1)}, u32[]{:S(2)}) copy-start(bf16[2048,64]{0,1:T(8,128)(2,1)} %param.11) | copy-start | bytes 786436
Sparse Core Ops, SparseCore 0:
  8.9 173.9 all-gather.2

commit v3 on v2

v3 whole, which is shorter than its diff:
```python
import functools

import jax
import jax.numpy as jnp
from jax import lax
from jax.experimental import pallas as pl
from jax.experimental.pallas import tpu as pltpu
from jax.sharding import PartitionSpec as P

ROUTE_SCALE = 2.5
MESH = pl.DeviceIdType.MESH


def ring_of(idx):
    z, y, core = idx // 4, (idx // 2) % 2, idx % 2
    return (z + y * (7 - 2 * z)) * 2 + core


def index_of(pos):
    pos = (pos + 32) % 16
    chip, core = pos // 2, pos % 2
    back = chip // 4
    z = chip + back * (7 - 2 * chip)
    return z * 4 + back * 2 + core


def gather_kernel(tok_hbm, meta_hbm, gate_hbm, up_hbm, shg_hbm, shu_hbm, shd_hbm, hid_hbm, all_meta_hbm, z_hbm,
                  tok_v, meta_v, rows_v, w_v, h_v, z_v,
                  tok_sem, own_sem, w_sem, h_sem, z_sem, keep_sem, send_sem, recv_sem, msend_sem, mrecv_sem):
    ring, _, sub_rows, hidden = tok_v.shape
    dev_slots = rows_v.shape[0]
    ff = h_v.shape[2]
    tok_count = 2 * sub_rows
    slot_cap = hid_hbm.shape[2]
    pair_rows = dev_slots * slot_cap
    bufs = w_v.shape[0]
    tiles = ff // 128
    far = ring // 2
    chunks = ring - 1
    me = lax.axis_index('ep')
    pos = ring_of(me)
    ahead = (index_of(pos + 1), index_of(pos - 1))
    col_tile = min(512, hidden)

    barrier = pltpu.get_barrier_semaphore()
    for off in range(1, ring):
        pl.semaphore_signal(barrier, inc=1, device_id={'ep': index_of(pos + off)}, device_id_type=MESH)

    own_meta = pltpu.make_async_copy(meta_hbm, meta_v.at[0], own_sem.at[0])
    own_toks = [pltpu.make_async_copy(tok_hbm.at[pl.ds(sub * sub_rows, sub_rows)], tok_v.at[0, sub], tok_sem.at[sub]) for sub in (0, 1)]
    own_meta.start()
    for copy in own_toks:
        copy.start()

    def chunk(i, way):
        dist = (i + 1) // 2
        sub = way if isinstance(i, int) and i == chunks else (i + 1) % 2
        if way == 0:
            src, dst = (ring + 1 - dist) % ring, ring - dist
        else:
            src, dst = dist - 1, dist
        return pltpu.make_async_remote_copy(
            src_ref=tok_v.at[src, sub], dst_ref=tok_v.at[dst, sub],
            send_sem=send_sem.at[way, i - 1], recv_sem=recv_sem.at[way, i - 1],
            device_id={'ep': ahead[way]}, device_id_type=MESH)

    def tick(i):
        for way in (0, 1):
            chunk(i, way).wait_recv()
            chunk(i + 2, way).start()

    def meta_copy(off):
        return pltpu.make_async_remote_copy(
            src_ref=meta_v.at[0], dst_ref=meta_v.at[ring - off],
            send_sem=msend_sem.at[off - 1], recv_sem=mrecv_sem.at[ring - off - 1],
            device_id={'ep': index_of(pos + off)}, device_id_type=MESH)

    def stream(copies_of, use, low, high, total):
        def body(i, _):
            for copy in copies_of(i):
                copy.wait()
            use(i, i % bufs)

            @pl.when(i + bufs < total)
            def _():
                for copy in copies_of(i + bufs):
                    copy.start()
            return 0
        lax.fori_loop(low, high, body, 0)

    def open_stream(copies_of):
        for i in range(bufs):
            for copy in copies_of(i):
                copy.start()

    def shared_copies(i):
        cols = pl.ds(pl.multiple_of(i * 128, 128), 128)
        return (pltpu.make_async_copy(shg_hbm.at[:, cols], w_v.at[i % bufs, :, pl.ds(0, 128)], w_sem.at[i % bufs, 0]),
                pltpu.make_async_copy(shu_hbm.at[:, cols], w_v.at[i % bufs, :, pl.ds(128, 128)], w_sem.at[i % bufs, 1]))

    def shared_use(i, buf):
        cols = pl.ds(pl.multiple_of(i % tiles * 128, 128), 128)
        for sub in (0, 1):
            both = jnp.dot(tok_v[0, sub], w_v[buf], preferred_element_type=jnp.float32)
            h_v[i // tiles, sub * sub_rows:(sub + 1) * sub_rows, cols] = (jax.nn.silu(both[:, :128]) * both[:, 128:]).astype(jnp.bfloat16)

    def last_copies(i):
        cols = pl.ds(pl.multiple_of(i // 2 * 256, 256), 256)
        rows = pl.ds(pl.multiple_of(i % 2 * ff, 128), ff)
        return (pltpu.make_async_copy(shd_hbm.at[rows, cols], w_v.at[i % bufs, pl.ds(0, ff), :], w_sem.at[i % bufs, 0]),)

    def z_copy(tile):
        cols = pl.ds(pl.multiple_of(tile * 256, 256), 256)
        return pltpu.make_async_copy(z_v.at[tile % 2], z_hbm.at[:, cols], z_sem.at[tile % 2])

    def last_use(i, buf):
        tile = i // 2
        part = jnp.dot(h_v[i % 2, :tok_count, :], w_v[buf, :ff, :], preferred_element_type=jnp.float32)

        @pl.when(i % 2 == 0)
        def _():
            @pl.when(tile >= 2)
            def _():
                z_copy(tile - 2).wait()
            z_v[tile % 2] = part

        @pl.when(i % 2 == 1)
        def _():
            z_v[tile % 2] += part
            z_copy(tile).start()

    def slot_copies(i):
        slot, tile = i // tiles, i % tiles
        cols = pl.ds(pl.multiple_of(tile * 128, 128), 128)
        return (pltpu.make_async_copy(gate_hbm.at[slot, :, cols], w_v.at[i % bufs, :, pl.ds(0, 128)], w_sem.at[i % bufs, 0]),
                pltpu.make_async_copy(up_hbm.at[slot, :, cols], w_v.at[i % bufs, :, pl.ds(128, 128)], w_sem.at[i % bufs, 1]))

    def slot_use(count):
        def use(i, buf):
            slot, tile = i // tiles, i % tiles
            both = jnp.dot(rows_v[slot, :count * slot_cap, :], w_v[buf], preferred_element_type=jnp.float32)
            cols = pl.ds(pl.multiple_of(tile * 128, 128), 128)
            h_v[slot % 2, :count * slot_cap, cols] = (jax.nn.silu(both[:, :128]) * both[:, 128:]).astype(jnp.bfloat16)
        return use

    def dispatch(block, place):
        ids = (lax.broadcasted_iota(jnp.int32, (pair_rows, 1), 0) + me * pair_rows).astype(jnp.float32)
        hit = meta_v[block, 0:1, :] == ids
        for j in range(1, 6):
            hit = hit | (meta_v[block, j:j + 1, :] == ids)
        pick = hit.astype(jnp.float32).astype(jnp.bfloat16)

        def one_tile(tile, _):
            cols = pl.ds(pl.multiple_of(tile * col_tile, col_tile), col_tile)
            rows = jnp.dot(pick[:, :sub_rows], tok_v[block, 0, :, cols], preferred_element_type=jnp.float32)
            rows += jnp.dot(pick[:, sub_rows:], tok_v[block, 1, :, cols], preferred_element_type=jnp.float32)
            rows = rows.astype(jnp.bfloat16)
            at = pl.multiple_of(place * slot_cap, 16)
            for slot in range(dev_slots):
                rows_v[slot, pl.ds(at, slot_cap), cols] = rows[slot * slot_cap:(slot + 1) * slot_cap]
            return 0
        lax.fori_loop(0, hidden // col_tile, one_tile, 0)

    near = [0] + [r for dist in range(1, far // 2 + 1) for r in (ring - dist, dist)]
    away = [r for dist in range(far // 2 + 1, far) for r in (ring - dist, dist)] + [far]

    def group(blocks, tick_from):
        def hid_copies(slot):
            return [pltpu.make_async_copy(h_v.at[slot % 2, pl.ds(k * slot_cap, slot_cap), :], hid_hbm.at[slot, r], h_sem.at[slot % 2, k])
                    for k, r in enumerate(blocks)]

        def one_slot(slot, _):
            @pl.when(slot >= 2)
            def _():
                for copy in hid_copies(slot - 2):
                    copy.wait()
            stream(slot_copies, slot_use(len(blocks)), slot * tiles, (slot + 1) * tiles, dev_slots * tiles)
            for copy in hid_copies(slot):
                copy.start()
            if tick_from is not None:
                @pl.when(slot < 4)
                def _():
                    tick(tick_from + slot)
            return 0
        lax.fori_loop(0, dev_slots, one_slot, 0)
        for slot in (dev_slots - 2, dev_slots - 1):
            for copy in hid_copies(slot):
                copy.wait()

    open_stream(shared_copies)
    own_meta.wait()
    for copy in own_toks:
        copy.wait()
    pl.semaphore_wait(barrier, ring - 1)
    for off in range(1, ring):
        meta_copy(off).start()
    for i in (1, 2):
        for way in (0, 1):
            chunk(i, way).start()
    stream(shared_copies, shared_use, 0, tiles, 2 * tiles)
    tick(1)
    stream(shared_copies, shared_use, tiles, 2 * tiles, 2 * tiles)
    open_stream(last_copies)
    for off in range(1, ring):
        meta_copy(off).wait_recv()
    keep = pltpu.make_async_copy(meta_v, all_meta_hbm, keep_sem)
    keep.start()
    tick(2)
    downs = 2 * (hidden // 256)
    stream(last_copies, last_use, 0, downs, downs)
    tick(3)
    open_stream(slot_copies)
    for tile in (hidden // 256 - 2, hidden // 256 - 1):
        z_copy(tile).wait()
    tick(4)
    dispatch(0, 0)

    def one_pair(dist, _):
        @pl.when(dist >= 3)
        def _():
            tick(2 * dist - 1)
            tick(2 * dist)
        dispatch(ring - dist, 2 * dist - 1)
        dispatch(dist, 2 * dist)
        return 0
    lax.fori_loop(1, far // 2 + 1, one_pair, 0)
    group(near, 2 * (far // 2) + 1)
    open_stream(slot_copies)

    def far_pair(dist, _):
        dispatch(ring - dist, 2 * dist - far - 2)
        dispatch(dist, 2 * dist - far - 1)
        return 0
    lax.fori_loop(far // 2 + 1, far - 1, far_pair, 0)
    chunk(chunks - 2, 0).wait_recv()
    chunk(chunks - 2, 1).wait_recv()
    chunk(chunks, 0).start()
    chunk(chunks - 1, 0).wait_recv()
    chunk(chunks - 1, 1).wait_recv()
    chunk(chunks, 1).start()
    far_pair(far - 1, 0)
    chunk(chunks, 0).wait_recv()
    chunk(chunks, 1).wait_recv()
    dispatch(far, far - 2)
    group(away, None)
    keep.wait()
    for off in range(1, ring):
        meta_copy(off).wait_send()
    for i in range(1, ring):
        for way in (0, 1):
            chunk(i, way).wait_send()


def gather_rows(tok_rows, meta, w_gate, w_up, sh_gate, sh_up, sh_down, ring, slot_cap):
    tok_count, hidden = tok_rows.shape
    dev_slots, _, ff = w_gate.shape
    any_spec = pl.BlockSpec(memory_space=pl.ANY)
    dma = pltpu.SemaphoreType.DMA
    near = ring // 2 + 1
    flops = 4 * hidden * ff * ring * dev_slots * slot_cap + 12 * tok_count * hidden * ff
    return pl.pallas_call(
        gather_kernel,
        out_shape=(jax.ShapeDtypeStruct((dev_slots, ring, slot_cap, ff), jnp.bfloat16),
                   jax.ShapeDtypeStruct((ring,) + meta.shape, jnp.float32),
                   jax.ShapeDtypeStruct((tok_count, hidden), jnp.float32)),
        in_specs=[any_spec] * 7,
        out_specs=(any_spec,) * 3,
        scratch_shapes=[
            pltpu.VMEM((ring, 2, tok_count // 2, hidden), jnp.bfloat16),
            pltpu.VMEM((ring,) + meta.shape, jnp.float32),
            pltpu.VMEM((dev_slots, near * slot_cap, hidden), jnp.bfloat16),
            pltpu.VMEM((4, hidden, 256), jnp.bfloat16),
            pltpu.VMEM((2, near * slot_cap, ff), jnp.bfloat16),
            pltpu.VMEM((2, tok_count, 256), jnp.float32),
            dma((2,)), dma((1,)), dma((4, 2)), dma((2, near)), dma((2,)), dma,
            dma((2, ring - 1)), dma((2, ring - 1)), dma((ring - 1,)), dma((ring - 1,)),
        ],
        compiler_params=pltpu.CompilerParams(collective_id=2, has_side_effects=True, vmem_limit_bytes=66_000_000),
        cost_estimate=pl.CostEstimate(flops=flops, bytes_accessed=170_000_000, transcendentals=0),
        name='gather_rows',
    )(tok_rows, meta, w_gate, w_up, sh_gate, sh_up, sh_down)


def reduce_kernel(hid_hbm, meta_hbm, down_hbm, out_hbm, down_v, hid_v, meta_v, weigh_v, tri_v, own_v, run_v,
                  down_sem, hid_sem, meta_sem, send_sem, recv_sem, free_sem, out_sem):
    steps = meta_hbm.shape[0]
    dev_slots, slot_cap, _ = hid_v.shape[2:]
    pair_rows = dev_slots * slot_cap
    half = run_v.shape[4]
    sub_rows = run_v.shape[3]
    col_tile = min(512, half)
    mix_tile = min(256, half)
    tok_tile = min(128, 2 * sub_rows)
    wide = weigh_v.shape[1] // 3
    me = lax.axis_index('ep')
    pos = ring_of(me)
    ahead = (index_of(pos + 1), index_of(pos - 1))
    behind = (index_of(pos - 1), index_of(pos + 1))

    barrier = pltpu.get_barrier_semaphore()
    for peer in ahead:
        pl.semaphore_signal(barrier, inc=1, device_id={'ep': peer}, device_id_type=MESH)

    def block_of(step, way):
        return steps - 1 - step if way == 0 else (step + 1) % steps

    def fetches(step, way):
        par = step % 2
        block = block_of(step, way)
        return (pltpu.make_async_copy(hid_hbm.at[:, block], hid_v.at[par, way], hid_sem.at[par, way]),
                pltpu.make_async_copy(meta_hbm.at[block], meta_v.at[par, way], meta_sem.at[par, way]))

    def start_fetch(step):
        for way in (0, 1):
            for copy in fetches(step, way):
                copy.start()

    def down_copy(slot):
        return pltpu.make_async_copy(down_hbm.at[slot], down_v.at[slot], down_sem.at[slot])

    def build_weigh(par, way):
        lane = lax.broadcasted_iota(jnp.int32, (1, wide), 1)
        ids = jnp.where(lane < pair_rows, lane + me * pair_rows, -1).astype(jnp.float32)

        def one_tile(tile, _):
            toks = pl.ds(pl.multiple_of(tile * tok_tile, tok_tile), tok_tile)
            info = jnp.transpose(meta_v[par, way, :, toks])
            weigh = jnp.zeros((tok_tile, wide), jnp.float32)
            for j in range(6):
                weigh = jnp.where(info[:, j:j + 1] == ids, info[:, 6 + j:7 + j], weigh)
            hi = weigh.astype(jnp.bfloat16)
            rest = weigh - hi.astype(jnp.float32)
            mid = rest.astype(jnp.bfloat16)
            low = (rest - mid.astype(jnp.float32)).astype(jnp.bfloat16)
            weigh_v[toks, :wide] = low
            weigh_v[toks, wide:2 * wide] = mid
            weigh_v[toks, 2 * wide:] = hi
            return 0
        lax.fori_loop(0, 2 * sub_rows // tok_tile, one_tile, 0)

    def compute_own(step, first=False):
        par = step % 2
        for way in (0, 1):
            for copy in fetches(step, way):
                copy.wait()
            build_weigh(par, way)

            def one_slot(slot, _):
                if first and way == 0:
                    down_copy(slot).wait()
                for col in range(0, half, col_tile):
                    rows = jnp.dot(hid_v[par, way, slot], down_v[slot, :, way * half + col:way * half + col + col_tile],
                                   preferred_element_type=jnp.float32).astype(jnp.bfloat16)
                    for part in range(3):
                        at = pl.multiple_of(slot * slot_cap + part * wide, 16)
                        tri_v[pl.ds(at, slot_cap), col:col + col_tile] = rows
                return 0

            lax.fori_loop(0, dev_slots, one_slot, 0)

            def one_tile(tile, _):
                cols = pl.ds(pl.multiple_of(tile * mix_tile, mix_tile), mix_tile)
                own_v[way, :, cols] = jnp.dot(weigh_v[...], tri_v[:, cols], preferred_element_type=jnp.float32)
                return 0

            lax.fori_loop(0, half // mix_tile, one_tile, 0)

    def send(step, way, sub):
        now, later = step % 2, (step + 1) % 2
        return pltpu.make_async_remote_copy(
            src_ref=run_v.at[way, now, sub], dst_ref=run_v.at[way, later, sub],
            send_sem=send_sem.at[way, now, sub], recv_sem=recv_sem.at[way, later, sub],
            device_id={'ep': ahead[way]}, device_id_type=MESH)

    start_fetch(0)
    for slot in range(dev_slots):
        down_copy(slot).start()
    start_fetch(1)
    tri_v[...] = jnp.zeros_like(tri_v)
    compute_own(0, True)
    start_fetch(2)
    pl.semaphore_wait(barrier, 2)
    for sub in (0, 1):
        for way in (0, 1):
            run_v[way, 0, sub] = own_v[way, sub * sub_rows:(sub + 1) * sub_rows, :]
            send(0, way, sub).start()
    compute_own(1)
    start_fetch(3)

    def one_step(step, _):
        now = step % 2
        for sub in (0, 1):
            for way in (0, 1):
                send(step - 1, way, sub).wait_recv()
                send(step - 1, way, sub).wait_send()
                pl.semaphore_signal(free_sem.at[way, sub], inc=1, device_id={'ep': behind[way]}, device_id_type=MESH)
                run_v[way, now, sub] += own_v[way, sub * sub_rows:(sub + 1) * sub_rows, :]
                pl.semaphore_wait(free_sem.at[way, sub], 1)
                send(step, way, sub).start()
        compute_own(step + 1)

        @pl.when(step + 3 < steps)
        def _():
            start_fetch(step + 3)
        return 0

    lax.fori_loop(1, steps - 1, one_step, 0)
    last = (steps - 1) % 2
    outs = []
    for sub in (0, 1):
        for way in (0, 1):
            send(steps - 2, way, sub).wait_recv()
            send(steps - 2, way, sub).wait_send()
            run_v[way, last, sub] += own_v[way, sub * sub_rows:(sub + 1) * sub_rows, :]
            outs.append(pltpu.make_async_copy(run_v.at[way, last, sub],
                                              out_hbm.at[pl.ds(sub * sub_rows, sub_rows), pl.ds(way * half, half)],
                                              out_sem.at[way, sub]))
            outs[-1].start()
    for copy in outs:
        copy.wait()


def reduce_home(hid, meta, w_down):
    dev_slots, steps, slot_cap, ff = hid.shape
    tok_count = meta.shape[2]
    wide = (dev_slots * slot_cap + 127) // 128 * 128
    hidden = w_down.shape[2]
    half, sub_rows = hidden // 2, tok_count // 2
    any_spec = pl.BlockSpec(memory_space=pl.ANY)
    dma = pltpu.SemaphoreType.DMA
    flops = 2 * steps * dev_slots * slot_cap * hidden * (ff + 3 * tok_count)
    return pl.pallas_call(
        reduce_kernel,
        out_shape=jax.ShapeDtypeStruct((tok_count, hidden), jnp.float32),
        in_specs=[any_spec] * 3,
        out_specs=any_spec,
        scratch_shapes=[
            pltpu.VMEM((dev_slots, ff, hidden), jnp.bfloat16),
            pltpu.VMEM((2, 2, dev_slots, slot_cap, ff), jnp.bfloat16),
            pltpu.VMEM((2, 2) + meta.shape[1:], jnp.float32),
            pltpu.VMEM((tok_count, 3 * wide), jnp.bfloat16),
            pltpu.VMEM((3 * wide, half), jnp.bfloat16),
            pltpu.VMEM((2, tok_count, half), jnp.float32),
            pltpu.VMEM((2, 2, 2, sub_rows, half), jnp.float32),
            dma((dev_slots,)), dma((2, 2)), dma((2, 2)), dma((2, 2, 2)), dma((2, 2, 2)),
            pltpu.SemaphoreType.REGULAR((2, 2)), dma((2, 2)),
        ],
        compiler_params=pltpu.CompilerParams(collective_id=1, has_side_effects=True, vmem_limit_bytes=65_000_000),
        cost_estimate=pl.CostEstimate(flops=flops, bytes_accessed=70_000_000, transcendentals=0),
        name='reduce_home',
    )(hid, meta, w_down)


def solution(mesh):
    ep_size = mesh.shape['ep']

    def local_block(tok_rows, router_w, top_idx, slot_idx, w_gate, w_up, w_down, sh_gate, sh_up, sh_down):
        tok_count = tok_rows.shape[0]
        top_k = top_idx.shape[1]
        dev_slots = w_gate.shape[0]
        num_slots = ep_size * dev_slots
        slot_cap = ((2 * tok_count * top_k + num_slots - 1) // num_slots + 15) // 16 * 16
        logits = jnp.dot(tok_rows, router_w, preferred_element_type=jnp.float32)
        scores = jax.nn.sigmoid(logits)
        exp_ids = jnp.arange(router_w.shape[1], dtype=jnp.int32)
        picked = jnp.sum(jnp.where(top_idx[:, :, None] == exp_ids, scores[:, None, :], 0.0), axis=2)
        gate_wts = picked / jnp.sum(picked, axis=1, keepdims=True) * ROUTE_SCALE
        match = slot_idx[:, :, None] == jnp.arange(num_slots, dtype=jnp.int32)
        hot = jnp.any(match, axis=1)
        before = (jnp.arange(tok_count)[:, None] > jnp.arange(tok_count)[None, :]).astype(jnp.bfloat16)
        rank = jnp.dot(before, hot.astype(jnp.bfloat16), preferred_element_type=jnp.float32)
        dest = slot_idx.astype(jnp.float32) * slot_cap + jnp.sum(jnp.where(match, rank[:, None, :], 0.0), axis=2)
        meta = jnp.concatenate([dest, gate_wts, jnp.zeros((tok_count, 16 - 2 * top_k), jnp.float32)], axis=1).T
        hid, all_meta, shared_out = gather_rows(tok_rows, meta, w_gate, w_up, sh_gate, sh_up, sh_down, ep_size, slot_cap)
        routed = reduce_home(hid, all_meta, w_down)
        return (shared_out + routed).astype(jnp.bfloat16)

    tok_spec = P(('dp', 'ep'), None)
    slot_spec = P('ep', None, None)
    return jax.shard_map(local_block, mesh=mesh,
                         in_specs=(tok_spec, P(None, None), tok_spec, tok_spec, slot_spec, slot_spec, slot_spec,
                                   P(None, None), P(None, None), P(None, None)),
                         out_specs=tok_spec, check_vma=False)
```

time: 715 us -> 609 us (0.85)
  Pallas kernels: 363 us -> 594 us
  matrix products: 175 us -> 2.65 us
  waiting for transfers between devices: 81.3 us -> 0 us
  local copies, waits for them, and re-layouts: 35.7 us -> 0.09 us
  blocking collectives: 27.6 us -> 0 us
  between operations: 13.5 us -> 0.06 us
  other arithmetic: 18 us -> 9.37 us
    pallas_call x0 -> x1, Pallas kernels: none -> 231 us  [gather_rows(): pl.pallas_call(gather_kernel, out_shape=(jax.ShapeDtypeStruct((dev_slots,...]
    dot_general x6 -> x1, matrix products: 173 us -> 0.27 us  [local_block(): jnp.dot(before, hot.astype(jnp.bfloat16), preferred_element_type=jnp.floa...]
    all_gather x1 -> x0, waiting for transfers between devices: 80.6 us -> none  [local_block(): all_rows = lax.all_gather(tok_rows, 'ep', axis=0, tiled=False)]
    concatenate x1, local copies, waits for them, and re-layouts: 35.5 us -> 0.08 us  [local_block(): jnp.concatenate([dest, gate_wts, jnp.zeros((tok_count, 16 - 2 * top_k), j...]
    all_gather x1 -> x0, blocking collectives: 27.6 us -> none  [local_block(): all_meta = lax.all_gather(meta, 'ep', axis=0, tiled=True)]
    convert_element_type x2 -> x1, other arithmetic: 16.1 us -> 5.41 us  [local_block(): return (shared_out + routed).astype(jnp.bfloat16)]
  transfers between devices with their start and end apart: 1 -> 0, of which waited for: 1 -> 0; matrix products, arithmetic and copies ran while one was open for 9% -> 0% of each run, Pallas kernels for 0% -> 0%
where the time goes in v3:
time: 609 us; the launch traced here: 606 us
  Pallas kernels  594 us (98%)
  other arithmetic  9.37 us (2%)
    pallas_call x1, Pallas kernels, reduce_home(): pl.pallas_call(reduce_kernel, out_shape=jax.ShapeDtypeStruct((tok_count,...  363 us
    pallas_call x1, Pallas kernels, gather_rows(): pl.pallas_call(gather_kernel, out_shape=(jax.ShapeDtypeStruct((dev_slots,...  231 us

profile of v3, /device:TPU:0, one launch (start us, length us, event | category | flops | bytes accessed | tf_op | source)
XLA Modules:
  0.0 605.9 jit_solution(9872523805040937781)
XLA Ops:
  0.0 0.0 copy-start
  0.0 0.1 pad.2.clone
  0.1 0.8 fusion.4
  0.9 0.3 fusion.3
  1.2 0.8 select_reduce_fusion.2
  2.0 0.0 copy-done
  2.1 2.4 fusion.2
  4.4 0.9 select_reduce_fusion
  5.3 0.7 divide_multiply_fusion
  6.0 0.7 maximum_bitcast_fusion.meta_hbm
  6.7 230.7 %gather_rows.1 = (bf16[5,16,80,1408]{3,2,1,0:T(8,128)(2,1)}, f32[16,16,512]{2,1,0:T(8,128)}, f32[512,2048]{1,0:T(8,128)}) custom-call(bf16[512,2048]{1,0:T(8,128)(2,1)} %tok_hbm.1, f32[16,512]{1,0:T(8,128)} %maximum_bitcast_fusion.meta_hbm, bf16[5,2048,1408]{2,1,0:T(8,128)(2,1)} %gate_hbm.1, bf16[5,2048,1408]{2,1,0:T(8,128)(2,1)} %up_hbm.1, ...), custom_call_target="tpu_custom_call" | custom-call | flops 91536490496 | bytes 170000000 | tf_op jit(solution)/shard_map/gather_rows/pallas_call | solution.py:261
  237.5 0.0 copy-start.1
  237.5 363.0 %reduce_home.1 = f32[512,2048]{1,0:T(8,128)} custom-call(bf16[5,16,80,1408]{3,2,1,0:T(8,128)(2,1)} %get-tuple-element.9.hid_hbm, f32[16,16,512]{2,1,0:T(8,128)} %get-tuple-element.10.meta_hbm, bf16[5,1408,2048]{2,1,0:T(8,128)(2,1)} %down_hbm.1), custom_call_target="tpu_custom_call" | custom-call | flops 77175193600 | bytes 70000000 | tf_op jit(solution)/shard_map/reduce_home/pallas_call | solution.py:432
  600.5 5.4 add_convert_fusion
  605.9 0.0 copy-done.1
  (1 shorter events, 0.0 us)
Async XLA Ops:
  0.0 2.1 copy-start
  237.5 368.5 %copy-start.1 = (bf16[2048,64]{0,1:T(8,128)(2,1)S(1)}, bf16[2048,64]{0,1:T(8,128)(2,1)}, u32[]{:S(2)}) copy-start(bf16[2048,64]{0,1:T(8,128)(2,1)} %param.11) | copy-start | bytes 786436

commit v4 on v3

v4 whole, which is shorter than its diff:
```python
import functools

import jax
import jax.numpy as jnp
from jax import lax
from jax.experimental import pallas as pl
from jax.experimental.pallas import tpu as pltpu
from jax.sharding import PartitionSpec as P

ROUTE_SCALE = 2.5
MESH = pl.DeviceIdType.MESH


def ring_of(idx):
    z, y, core = idx // 4, (idx // 2) % 2, idx % 2
    return (z + y * (7 - 2 * z)) * 2 + core


def index_of(pos):
    pos = (pos + 32) % 16
    chip, core = pos // 2, pos % 2
    back = chip // 4
    z = chip + back * (7 - 2 * chip)
    return z * 4 + back * 2 + core


SEG = 12


def slot_stream(gate_hbm, up_hbm, down_hbm, rows_v, w_v, h_v, y_v, y_hbm, w_sem, y_sem):
    dev_slots, rows = rows_v.shape[:2]
    ff = h_v.shape[1]
    bufs = w_v.shape[0]
    ups, downs = ff // 128, rows_v.shape[2] // 256
    per_slot = ups + downs
    total = dev_slots * per_slot
    slot_cap = y_v.shape[2]

    def up_copies(i):
        slot, tile = i // per_slot, i % per_slot
        cols = pl.ds(pl.multiple_of(tile * 128, 128), 128)
        return (pltpu.make_async_copy(gate_hbm.at[slot, :, cols], w_v.at[i % bufs, :, pl.ds(0, 128)], w_sem.at[i % bufs, 0]),
                pltpu.make_async_copy(up_hbm.at[slot, :, cols], w_v.at[i % bufs, :, pl.ds(128, 128)], w_sem.at[i % bufs, 1]))

    def down_copies(i):
        slot, tile = i // per_slot, i % per_slot - ups
        cols = pl.ds(pl.multiple_of(tile * 256, 256), 256)
        return (pltpu.make_async_copy(down_hbm.at[slot, :, cols], w_v.at[i % bufs, pl.ds(0, ff), :], w_sem.at[i % bufs, 0]),)

    def fetch(i):
        @pl.when(i % per_slot < ups)
        def _():
            for copy in up_copies(i):
                copy.start()

        @pl.when(i % per_slot >= ups)
        def _():
            for copy in down_copies(i):
                copy.start()

    def y_copy(slot, tile):
        cols = pl.ds(pl.multiple_of(tile * 256, 256), 256)
        at = pl.ds(pl.multiple_of(slot * slot_cap, 16), slot_cap)
        return pltpu.make_async_copy(y_v.at[tile % 2], y_hbm.at[:, at, cols], y_sem.at[tile % 2])

    def one(i, _):
        slot, k, buf = i // per_slot, i % per_slot, i % bufs

        @pl.when(k < ups)
        def _():
            for copy in up_copies(i):
                copy.wait()
            both = jnp.dot(rows_v[slot], w_v[buf], preferred_element_type=jnp.float32)
            cols = pl.ds(pl.multiple_of(k * 128, 128), 128)
            h_v[:rows, cols] = (jax.nn.silu(both[:, :128]) * both[:, 128:]).astype(jnp.bfloat16)

        @pl.when(k >= ups)
        def _():
            for copy in down_copies(i):
                copy.wait()
            tile = k - ups

            @pl.when((slot > 0) | (tile >= 2))
            def _():
                y_copy(slot, tile).wait()
            outs = jnp.dot(h_v[:rows, :], w_v[buf, :ff, :], preferred_element_type=jnp.float32).astype(jnp.bfloat16)
            y_v[tile % 2] = outs.reshape(rows // slot_cap, slot_cap, 256)
            y_copy(slot, tile).start()

        @pl.when(i + bufs < total)
        def _():
            fetch(i + bufs)
        return 0

    def open_all():
        for i in range(bufs):
            fetch(jnp.int32(i))

    def run(seg):
        lax.fori_loop(seg * SEG, jnp.minimum(seg * SEG + SEG, total), one, 0)

    def close():
        for tile in (downs - 2, downs - 1):
            y_copy(dev_slots - 1, tile).wait()

    return open_all, run, close, -(-total // SEG)


def gather_kernel(tok_hbm, meta_hbm, gate_hbm, up_hbm, down_hbm, shg_hbm, shu_hbm, shd_hbm, y_hbm, far_hbm, all_meta_hbm, z_hbm,
                  tok_v, meta_v, rows_v, far_v, w_v, h_v, y_v, z_v,
                  tok_sem, own_sem, w_sem, y_sem, far_sem, z_sem, keep_sem, send_sem, recv_sem, msend_sem, mrecv_sem):
    ring, _, sub_rows, hidden = tok_v.shape
    dev_slots = rows_v.shape[0]
    ff = h_v.shape[2]
    tok_count = 2 * sub_rows
    slot_cap = y_v.shape[2]
    pair_rows = dev_slots * slot_cap
    bufs = w_v.shape[0]
    tiles = ff // 128
    far = ring // 2
    chunks = ring - 1
    me = lax.axis_index('ep')
    pos = ring_of(me)
    ahead = (index_of(pos + 1), index_of(pos - 1))
    col_tile = min(512, hidden)

    barrier = pltpu.get_barrier_semaphore()
    for off in range(1, ring):
        pl.semaphore_signal(barrier, inc=1, device_id={'ep': index_of(pos + off)}, device_id_type=MESH)

    own_meta = pltpu.make_async_copy(meta_hbm, meta_v.at[0], own_sem.at[0])
    own_toks = [pltpu.make_async_copy(tok_hbm.at[pl.ds(sub * sub_rows, sub_rows)], tok_v.at[0, sub], tok_sem.at[sub]) for sub in (0, 1)]
    own_meta.start()
    for copy in own_toks:
        copy.start()

    def chunk(i, way):
        dist = (i + 1) // 2
        sub = (i + 1) % 2 + way * (i // chunks)
        if way == 0:
            src, dst = (ring + 1 - dist) % ring, ring - dist
        else:
            src, dst = dist - 1, dist
        return pltpu.make_async_remote_copy(
            src_ref=tok_v.at[src, sub], dst_ref=tok_v.at[dst, sub],
            send_sem=send_sem.at[way, i - 1], recv_sem=recv_sem.at[way, i - 1],
            device_id={'ep': ahead[way]}, device_id_type=MESH)

    def tick(i):
        for way in (0, 1):
            chunk(i, way).wait_recv()

            @pl.when(i <= chunks - 3)
            def _():
                chunk(i + 2, way).start()

            @pl.when(i == chunks - 2 + way)
            def _():
                chunk(chunks, way).start()

    def meta_copy(off):
        return pltpu.make_async_remote_copy(
            src_ref=meta_v.at[0], dst_ref=meta_v.at[ring - off],
            send_sem=msend_sem.at[off - 1], recv_sem=mrecv_sem.at[ring - off - 1],
            device_id={'ep': index_of(pos + off)}, device_id_type=MESH)

    def stream(copies_of, use, low, high, total):
        def body(i, _):
            for copy in copies_of(i):
                copy.wait()
            use(i, i % bufs)

            @pl.when(i + bufs < total)
            def _():
                for copy in copies_of(i + bufs):
                    copy.start()
            return 0
        lax.fori_loop(low, high, body, 0)

    def open_stream(copies_of):
        for i in range(bufs):
            for copy in copies_of(i):
                copy.start()

    def shared_copies(i):
        cols = pl.ds(pl.multiple_of(i * 128, 128), 128)
        return (pltpu.make_async_copy(shg_hbm.at[:, cols], w_v.at[i % bufs, :, pl.ds(0, 128)], w_sem.at[i % bufs, 0]),
                pltpu.make_async_copy(shu_hbm.at[:, cols], w_v.at[i % bufs, :, pl.ds(128, 128)], w_sem.at[i % bufs, 1]))

    def shared_use(i, buf):
        cols = pl.ds(pl.multiple_of(i % tiles * 128, 128), 128)
        for sub in (0, 1):
            both = jnp.dot(tok_v[0, sub], w_v[buf], preferred_element_type=jnp.float32)
            h_v[i // tiles, sub * sub_rows:(sub + 1) * sub_rows, cols] = (jax.nn.silu(both[:, :128]) * both[:, 128:]).astype(jnp.bfloat16)

    def last_copies(i):
        cols = pl.ds(pl.multiple_of(i // 2 * 256, 256), 256)
        rows = pl.ds(pl.multiple_of(i % 2 * ff, 128), ff)
        return (pltpu.make_async_copy(shd_hbm.at[rows, cols], w_v.at[i % bufs, pl.ds(0, ff), :], w_sem.at[i % bufs, 0]),)

    def z_copy(tile):
        cols = pl.ds(pl.multiple_of(tile * 256, 256), 256)
        return pltpu.make_async_copy(z_v.at[tile % 2], z_hbm.at[:, cols], z_sem.at[tile % 2])

    def last_use(i, buf):
        tile = i // 2
        part = jnp.dot(h_v[i % 2, :tok_count, :], w_v[buf, :ff, :], preferred_element_type=jnp.float32)

        @pl.when(i % 2 == 0)
        def _():
            @pl.when(tile >= 2)
            def _():
                z_copy(tile - 2).wait()
            z_v[tile % 2] = part

        @pl.when(i % 2 == 1)
        def _():
            z_v[tile % 2] += part
            z_copy(tile).start()

    def select(block, keep_rows):
        ids = (lax.broadcasted_iota(jnp.int32, (pair_rows, 1), 0) + me * pair_rows).astype(jnp.float32)
        hit = meta_v[block, 0:1, :] == ids
        for j in range(1, 6):
            hit = hit | (meta_v[block, j:j + 1, :] == ids)
        pick = hit.astype(jnp.float32).astype(jnp.bfloat16)

        def one_tile(tile, _):
            cols = pl.ds(pl.multiple_of(tile * col_tile, col_tile), col_tile)
            rows = jnp.dot(pick[:, :sub_rows], tok_v[block, 0, :, cols], preferred_element_type=jnp.float32)
            rows += jnp.dot(pick[:, sub_rows:], tok_v[block, 1, :, cols], preferred_element_type=jnp.float32)
            rows = rows.astype(jnp.bfloat16)
            for slot in range(dev_slots):
                keep_rows(slot, cols, rows[slot * slot_cap:(slot + 1) * slot_cap])
            return 0
        lax.fori_loop(0, hidden // col_tile, one_tile, 0)

    def dispatch(block, place):
        at = pl.multiple_of(place * slot_cap, 16)

        def keep_rows(slot, cols, rows):
            rows_v[slot, pl.ds(at, slot_cap), cols] = rows
        select(block, keep_rows)

    def far_copy(place):
        at = pl.ds(pl.multiple_of(place * slot_cap, 16), slot_cap)
        return pltpu.make_async_copy(far_v.at[place % 2], far_hbm.at[:, at, :], far_sem.at[place % 2])

    def far_dispatch(block, place):
        @pl.when(place >= 2)
        def _():
            far_copy(place - 2).wait()

        def keep_rows(slot, cols, rows):
            far_v[place % 2, slot, :, cols] = rows
        select(block, keep_rows)
        far_copy(place).start()

    open_slots, run_slots, close_slots, segs = slot_stream(
        gate_hbm, up_hbm, down_hbm, rows_v, w_v, h_v.at[0], y_v, y_hbm, w_sem, y_sem)

    open_stream(shared_copies)
    own_meta.wait()
    for copy in own_toks:
        copy.wait()
    pl.semaphore_wait(barrier, ring - 1)
    for off in range(1, ring):
        meta_copy(off).start()
    for i in (1, 2):
        for way in (0, 1):
            chunk(i, way).start()
    stream(shared_copies, shared_use, 0, tiles, 2 * tiles)
    tick(1)
    stream(shared_copies, shared_use, tiles, 2 * tiles, 2 * tiles)
    open_stream(last_copies)
    for off in range(1, ring):
        meta_copy(off).wait_recv()
    keep = pltpu.make_async_copy(meta_v, all_meta_hbm, keep_sem)
    keep.start()
    tick(2)
    downs = 2 * (hidden // 256)
    stream(last_copies, last_use, 0, downs, downs)
    tick(3)
    open_slots()
    for tile in (hidden // 256 - 2, hidden // 256 - 1):
        z_copy(tile).wait()
    tick(4)
    dispatch(0, 0)

    def one_pair(dist, _):
        @pl.when(dist >= 3)
        def _():
            tick(2 * dist - 1)
            tick(2 * dist)
        dispatch(ring - dist, 2 * dist - 1)
        dispatch(dist, 2 * dist)
        return 0
    lax.fori_loop(1, far // 2 + 1, one_pair, 0)
    left = chunks - far

    def one_seg(seg, _):
        @pl.when(seg < segs)
        def _():
            run_slots(seg)

        @pl.when(seg < left)
        def _():
            tick(far + 1 + seg)

        @pl.when((seg % 2 == 1) & (seg < left))
        def _():
            dist = far // 2 + 1 + seg // 2
            far_dispatch(ring - dist, seg - 1)
            far_dispatch(dist, seg)
        return 0
    lax.fori_loop(0, max(segs, left), one_seg, 0)
    far_dispatch(far, jnp.int32(far - 2))
    close_slots()
    far_copy(jnp.int32(far - 3)).wait()
    far_copy(jnp.int32(far - 2)).wait()
    keep.wait()
    for off in range(1, ring):
        meta_copy(off).wait_send()
    for i in range(1, ring):
        for way in (0, 1):
            chunk(i, way).wait_send()


def gather_rows(tok_rows, meta, w_gate, w_up, w_down, sh_gate, sh_up, sh_down, ring, slot_cap):
    tok_count, hidden = tok_rows.shape
    dev_slots, _, ff = w_gate.shape
    any_spec = pl.BlockSpec(memory_space=pl.ANY)
    dma = pltpu.SemaphoreType.DMA
    near = ring // 2 + 1
    flops = 6 * hidden * ff * near * dev_slots * slot_cap + 12 * tok_count * hidden * ff
    return pl.pallas_call(
        gather_kernel,
        out_shape=(jax.ShapeDtypeStruct((near, dev_slots * slot_cap, hidden), jnp.bfloat16),
                   jax.ShapeDtypeStruct((dev_slots, (ring - near) * slot_cap, hidden), jnp.bfloat16),
                   jax.ShapeDtypeStruct((ring,) + meta.shape, jnp.float32),
                   jax.ShapeDtypeStruct((tok_count, hidden), jnp.float32)),
        in_specs=[any_spec] * 8,
        out_specs=(any_spec,) * 4,
        scratch_shapes=[
            pltpu.VMEM((ring, 2, tok_count // 2, hidden), jnp.bfloat16),
            pltpu.VMEM((ring,) + meta.shape, jnp.float32),
            pltpu.VMEM((dev_slots, near * slot_cap, hidden), jnp.bfloat16),
            pltpu.VMEM((2, dev_slots, slot_cap, hidden), jnp.bfloat16),
            pltpu.VMEM((4, hidden, 256), jnp.bfloat16),
            pltpu.VMEM((2, near * slot_cap, ff), jnp.bfloat16),
            pltpu.VMEM((2, near, slot_cap, 256), jnp.bfloat16),
            pltpu.VMEM((2, tok_count, 256), jnp.float32),
            dma((2,)), dma((1,)), dma((4, 2)), dma((2,)), dma((2,)), dma((2,)), dma,
            dma((2, ring - 1)), dma((2, ring - 1)), dma((ring - 1,)), dma((ring - 1,)),
        ],
        compiler_params=pltpu.CompilerParams(collective_id=2, has_side_effects=True, vmem_limit_bytes=67_000_000),
        cost_estimate=pl.CostEstimate(flops=flops, bytes_accessed=170_000_000, transcendentals=0),
        name='gather_rows',
    )(tok_rows, meta, w_gate, w_up, w_down, sh_gate, sh_up, sh_down)


def reduce_kernel(near_hbm, x_hbm, meta_hbm, gate_hbm, up_hbm, down_hbm, out_hbm, far_hbm,
                  x_v, w_v, h_v, y_v, meta_v, weigh_v, tri_v, own_v, run_v,
                  x_sem, w_sem, y_sem, tri_sem, meta_sem, send_sem, recv_sem, free_sem, out_sem):
    steps = meta_hbm.shape[0]
    near = near_hbm.shape[0]
    pair_rows = near_hbm.shape[1]
    half = run_v.shape[4]
    sub_rows = run_v.shape[3]
    mix_tile = min(256, half)
    tok_tile = min(128, 2 * sub_rows)
    wide = weigh_v.shape[1] // 3
    early = near // 2
    me = lax.axis_index('ep')
    pos = ring_of(me)
    ahead = (index_of(pos + 1), index_of(pos - 1))
    behind = (index_of(pos - 1), index_of(pos + 1))

    barrier = pltpu.get_barrier_semaphore()
    for peer in ahead:
        pl.semaphore_signal(barrier, inc=1, device_id={'ep': peer}, device_id_type=MESH)

    def block_of(step, way):
        return steps - 1 - step if way == 0 else (step + 1) % steps

    def place_of(step, way):
        behind_half = (step + 1) // (steps // 2 + 1)
        dist = step + 1 + behind_half * (steps - 2 - 2 * step)
        side = way + behind_half * (1 - 2 * way)
        middle = dist // (steps // 2)
        last = (step + 1) // steps
        return (2 * dist - 1 + side) * (1 - middle) * (1 - last) + middle * (steps - 1)

    def meta_fetch(step, way):
        return pltpu.make_async_copy(meta_hbm.at[block_of(step, way)], meta_v.at[step % 2, way], meta_sem.at[step % 2, way])

    def tri_fetch(step, way, part, source, base):
        cols = pl.ds(way * half, half)
        return pltpu.make_async_copy(source.at[place_of(step, way) - base, :, cols],
                                     tri_v.at[step % 2, way, pl.ds(part * wide, pair_rows), :], tri_sem.at[step % 2, way, part])

    def wait_tri(par, way, part):
        pltpu.make_async_copy(near_hbm.at[0, :, pl.ds(way * half, half)],
                              tri_v.at[par, way, pl.ds(part * wide, pair_rows), :], tri_sem.at[par, way, part]).wait()

    def start_fetch(step, is_far):
        for way in (0, 1):
            meta_fetch(step, way).start()
            for part in range(3):
                tri_fetch(step, way, part, *((far_hbm, near) if is_far else (near_hbm, 0))).start()

    def build_weigh(par, way):
        lane = lax.broadcasted_iota(jnp.int32, (1, wide), 1)
        ids = jnp.where(lane < pair_rows, lane + me * pair_rows, -1).astype(jnp.float32)

        def one_tile(tile, _):
            toks = pl.ds(pl.multiple_of(tile * tok_tile, tok_tile), tok_tile)
            info = jnp.transpose(meta_v[par, way, :, toks])
            weigh = jnp.zeros((tok_tile, wide), jnp.float32)
            for j in range(6):
                weigh = jnp.where(info[:, j:j + 1] == ids, info[:, 6 + j:7 + j], weigh)
            hi = weigh.astype(jnp.bfloat16)
            rest = weigh - hi.astype(jnp.float32)
            mid = rest.astype(jnp.bfloat16)
            low = (rest - mid.astype(jnp.float32)).astype(jnp.bfloat16)
            weigh_v[toks, :wide] = low
            weigh_v[toks, wide:2 * wide] = mid
            weigh_v[toks, 2 * wide:] = hi
            return 0
        lax.fori_loop(0, 2 * sub_rows // tok_tile, one_tile, 0)

    def compute_own(step):
        par = step % 2
        for way in (0, 1):
            meta_fetch(step, way).wait()
            build_weigh(par, way)
            for part in range(3):
                wait_tri(par, way, part)

            def one_tile(tile, _):
                cols = pl.ds(pl.multiple_of(tile * mix_tile, mix_tile), mix_tile)
                own_v[way, :, cols] = jnp.dot(weigh_v[...], tri_v[par, way, :, cols], preferred_element_type=jnp.float32)
                return 0

            lax.fori_loop(0, half // mix_tile, one_tile, 0)

    def send(step, way, sub):
        now, later = step % 2, (step + 1) % 2
        return pltpu.make_async_remote_copy(
            src_ref=run_v.at[way, now, sub], dst_ref=run_v.at[way, later, sub],
            send_sem=send_sem.at[way, now, sub], recv_sem=recv_sem.at[way, later, sub],
            device_id={'ep': ahead[way]}, device_id_type=MESH)

    open_slots, run_slots, close_slots, segs = slot_stream(
        gate_hbm, up_hbm, down_hbm, x_v, w_v, h_v, y_v, far_hbm, w_sem, y_sem)
    per_step = -(-segs // (2 * early))

    for par in (0, 1):
        for way in (0, 1):
            for part in range(3):
                tri_v[par, way, part * wide + pair_rows:(part + 1) * wide, :] = jnp.zeros((wide - pair_rows, half), jnp.bfloat16)
    start_fetch(0, False)
    start_fetch(1, False)
    x_copy = pltpu.make_async_copy(x_hbm, x_v, x_sem)
    x_copy.start()
    open_slots()
    compute_own(0)
    start_fetch(2, False)
    pl.semaphore_wait(barrier, 2)
    for sub in (0, 1):
        for way in (0, 1):
            run_v[way, 0, sub] = own_v[way, sub * sub_rows:(sub + 1) * sub_rows, :]
            send(0, way, sub).start()
    x_copy.wait()

    def far_work(step, sub):
        for more in range(per_step):
            run_slots((2 * step + sub) * per_step + more)

    far_work(0, 0)
    compute_own(1)
    start_fetch(3, False)
    far_work(0, 1)

    def pass_on(step, sub):
        now = step % 2
        for way in (0, 1):
            send(step - 1, way, sub).wait_recv()
            send(step - 1, way, sub).wait_send()
            pl.semaphore_signal(free_sem.at[way, sub], inc=1, device_id={'ep': behind[way]}, device_id_type=MESH)
            run_v[way, now, sub] += own_v[way, sub * sub_rows:(sub + 1) * sub_rows, :]
            pl.semaphore_wait(free_sem.at[way, sub], 1)
            send(step, way, sub).start()

    def early_step(step, _):
        pass_on(step, 0)
        far_work(step, 0)
        pass_on(step, 1)
        far_work(step, 1)

        @pl.when(step == early - 1)
        def _():
            close_slots()
            start_fetch(early, True)
            start_fetch(early + 1, True)
        compute_own(step + 1)
        return 0

    lax.fori_loop(1, early, early_step, 0)
    start_fetch(early + 2, True)

    def late_step(step, _):
        pass_on(step, 0)
        pass_on(step, 1)
        compute_own(step + 1)
        ahead_far = step + 3 < steps - 1 - early

        @pl.when(ahead_far)
        def _():
            start_fetch(step + 3, True)

        @pl.when(jnp.logical_not(ahead_far) & (step + 3 < steps))
        def _():
            start_fetch(step + 3, False)
        return 0

    lax.fori_loop(early, steps - 1, late_step, 0)
    last = (steps - 1) % 2
    outs = []
    for sub in (0, 1):
        for way in (0, 1):
            send(steps - 2, way, sub).wait_recv()
            send(steps - 2, way, sub).wait_send()
            run_v[way, last, sub] += own_v[way, sub * sub_rows:(sub + 1) * sub_rows, :]
            outs.append(pltpu.make_async_copy(run_v.at[way, last, sub],
                                              out_hbm.at[pl.ds(sub * sub_rows, sub_rows), pl.ds(way * half, half)],
                                              out_sem.at[way, sub]))
            outs[-1].start()
    for copy in outs:
        copy.wait()


def reduce_home(near_out, far_rows, meta, w_gate, w_up, w_down):
    near, pair_rows, hidden = near_out.shape
    dev_slots, ff, _ = w_down.shape
    slot_cap = pair_rows // dev_slots
    steps, _, tok_count = meta.shape
    far = steps - near
    half, sub_rows = hidden // 2, tok_count // 2
    wide = (pair_rows + 127) // 128 * 128
    any_spec = pl.BlockSpec(memory_space=pl.ANY)
    dma = pltpu.SemaphoreType.DMA
    flops = 6 * far * pair_rows * hidden * ff + 6 * steps * pair_rows * hidden * tok_count
    return pl.pallas_call(
        reduce_kernel,
        out_shape=(jax.ShapeDtypeStruct((tok_count, hidden), jnp.float32),
                   jax.ShapeDtypeStruct((far, pair_rows, hidden), jnp.bfloat16)),
        in_specs=[any_spec] * 6,
        out_specs=(any_spec,) * 2,
        scratch_shapes=[
            pltpu.VMEM((dev_slots, far * slot_cap, hidden), jnp.bfloat16),
            pltpu.VMEM((4, hidden, 256), jnp.bfloat16),
            pltpu.VMEM((far * slot_cap, ff), jnp.bfloat16),
            pltpu.VMEM((2, far, slot_cap, 256), jnp.bfloat16),
            pltpu.VMEM((2, 2) + meta.shape[1:], jnp.float32),
            pltpu.VMEM((tok_count, 3 * wide), jnp.bfloat16),
            pltpu.VMEM((2, 2, 3 * wide, half), jnp.bfloat16),
            pltpu.VMEM((2, tok_count, half), jnp.float32),
            pltpu.VMEM((2, 2, 2, sub_rows, half), jnp.float32),
            dma, dma((4, 2)), dma((2,)), dma((2, 2, 3)), dma((2, 2)), dma((2, 2, 2)), dma((2, 2, 2)),
            pltpu.SemaphoreType.REGULAR((2, 2)), dma((2, 2)),
        ],
        compiler_params=pltpu.CompilerParams(collective_id=1, has_side_effects=True, vmem_limit_bytes=65_000_000),
        cost_estimate=pl.CostEstimate(flops=flops, bytes_accessed=170_000_000, transcendentals=0),
        name='reduce_home',
    )(near_out, far_rows, meta, w_gate, w_up, w_down)[0]


def solution(mesh):
    ep_size = mesh.shape['ep']

    def local_block(tok_rows, router_w, top_idx, slot_idx, w_gate, w_up, w_down, sh_gate, sh_up, sh_down):
        tok_count = tok_rows.shape[0]
        top_k = top_idx.shape[1]
        dev_slots = w_gate.shape[0]
        num_slots = ep_size * dev_slots
        slot_cap = ((2 * tok_count * top_k + num_slots - 1) // num_slots + 15) // 16 * 16
        logits = jnp.dot(tok_rows, router_w, preferred_element_type=jnp.float32)
        scores = jax.nn.sigmoid(logits)
        exp_ids = jnp.arange(router_w.shape[1], dtype=jnp.int32)
        picked = jnp.sum(jnp.where(top_idx[:, :, None] == exp_ids, scores[:, None, :], 0.0), axis=2)
        gate_wts = picked / jnp.sum(picked, axis=1, keepdims=True) * ROUTE_SCALE
        match = slot_idx[:, :, None] == jnp.arange(num_slots, dtype=jnp.int32)
        hot = jnp.any(match, axis=1)
        before = (jnp.arange(tok_count)[:, None] > jnp.arange(tok_count)[None, :]).astype(jnp.bfloat16)
        rank = jnp.dot(before, hot.astype(jnp.bfloat16), preferred_element_type=jnp.float32)
        dest = slot_idx.astype(jnp.float32) * slot_cap + jnp.sum(jnp.where(match, rank[:, None, :], 0.0), axis=2)
        meta = jnp.concatenate([dest, gate_wts, jnp.zeros((tok_count, 16 - 2 * top_k), jnp.float32)], axis=1).T
        near_out, far_rows, all_meta, shared_out = gather_rows(tok_rows, meta, w_gate, w_up, w_down, sh_gate, sh_up, sh_down, ep_size, slot_cap)
        routed = reduce_home(near_out, far_rows, all_meta, w_gate, w_up, w_down)
        return (shared_out + routed).astype(jnp.bfloat16)

    tok_spec = P(('dp', 'ep'), None)
    slot_spec = P('ep', None, None)
    return jax.shard_map(local_block, mesh=mesh,
                         in_specs=(tok_spec, P(None, None), tok_spec, tok_spec, slot_spec, slot_spec, slot_spec,
                                   P(None, None), P(None, None), P(None, None)),
                         out_specs=tok_spec, check_vma=False)
```

time: 609 us -> 609 us (level)
  no operation moved by 1% of the time
where the time goes in v4:
time: 609 us; the launch traced here: 606 us
  Pallas kernels  594 us (98%)
  other arithmetic  9.37 us (2%)
    pallas_call x1, Pallas kernels, reduce_home(): pl.pallas_call(reduce_kernel, out_shape=(jax.ShapeDtypeStruct((tok_count,...  384 us
    pallas_call x1, Pallas kernels, gather_rows(): pl.pallas_call(gather_kernel, out_shape=(jax.ShapeDtypeStruct((near, dev_...  210 us

profile of v4, /device:TPU:0, one launch (start us, length us, event | category | flops | bytes accessed | tf_op | source)
XLA Modules:
  0.0 606.0 jit_solution(1562092397270561031)
XLA Ops:
  0.0 0.1 pad.2.clone
  0.1 0.8 fusion.4
  0.9 0.3 fusion.3
  1.2 0.8 select_reduce_fusion.2
  2.0 2.4 fusion.2
  4.4 0.9 select_reduce_fusion
  5.3 0.7 divide_multiply_fusion
  6.0 0.7 maximum_bitcast_fusion.meta_hbm
  6.7 210.1 %gather_rows.1 = (bf16[9,400,2048]{2,1,0:T(8,128)(2,1)}, bf16[5,560,2048]{2,1,0:T(8,128)(2,1)}, f32[16,16,512]{2,1,0:T(8,128)}, f32[512,2048]{1,0:T(8,128)}) custom-call(bf16[512,2048]{1,0:T(8,128)(2,1)} %tok_hbm.1, f32[16,512]{1,0:T(8,128)} %maximum_bitcast_fusion.meta_hbm, bf16[5,2048,1408]{2,1,0:T(8,128)(2,1)} %gate_hbm.3, bf16[5,2048,1408]{2,1,0:T(8,128)(2,1)} %up_hbm.3, ...), custom_call_target="tpu_custom_call" | custom-call | flops 80002154496 | bytes 170000000 | tf_op jit(solution)/shard_map/gather_rows/pallas_call | solution.py:336
  216.9 383.7 %reduce_home.1 = (f32[512,2048]{1,0:T(8,128)}, bf16[7,400,2048]{2,1,0:T(8,128)(2,1)}) custom-call(bf16[9,400,2048]{2,1,0:T(8,128)(2,1)} %get-tuple-element.11.near_hbm, bf16[5,560,2048]{2,1,0:T(8,128)(2,1)} %get-tuple-element.12.x_hbm, f32[16,16,512]{2,1,0:T(8,128)} %get-tuple-element.13.meta_hbm, bf16[5,2048,1408]{2,1,0:T(8,128)(2,1)} %gate_hbm.3, ...), custom_call_target="tpu_custom_call" | custom-call | flops 88709529600 | bytes 170000000 | tf_op jit(solution)/shard_map/reduce_home/pallas_call | solution.py:554
  600.6 5.4 add_convert_fusion
  (1 shorter events, 0.0 us)

commit v5 on v4

--- a/solution.py
+++ b/solution.py
@@ -27,31 +27,47 @@
 SEG = 12
 
 
-def slot_stream(gate_hbm, up_hbm, down_hbm, rows_v, w_v, h_v, y_v, y_hbm, w_sem, y_sem):
+def slot_stream(gate_hbm, up_hbm, down_hbm, rows_v, w_v, g_v, h_v, y_v, y_hbm, w_sem, y_sem):
     dev_slots, rows = rows_v.shape[:2]
     ff = h_v.shape[1]
     bufs = w_v.shape[0]
+    whole = ff // 256 * 2
     ups, downs = ff // 128, rows_v.shape[2] // 256
     per_slot = ups + downs
     total = dev_slots * per_slot
     slot_cap = y_v.shape[2]
 
-    def up_copies(i):
+    def wide_copy(i, weight_hbm):
         slot, tile = i // per_slot, i % per_slot
-        cols = pl.ds(pl.multiple_of(tile * 128, 128), 128)
+        cols = pl.ds(pl.multiple_of(tile // 2 * 256, 256), 256)
+        return pltpu.make_async_copy(weight_hbm.at[slot, :, cols], w_v.at[i % bufs], w_sem.at[i % bufs, 0])
+
+    def pair_copies(i):
+        slot = i // per_slot
+        cols = pl.ds(whole * 128, 128)
         return (pltpu.make_async_copy(gate_hbm.at[slot, :, cols], w_v.at[i % bufs, :, pl.ds(0, 128)], w_sem.at[i % bufs, 0]),
                 pltpu.make_async_copy(up_hbm.at[slot, :, cols], w_v.at[i % bufs, :, pl.ds(128, 128)], w_sem.at[i % bufs, 1]))
 
     def down_copies(i):
         slot, tile = i // per_slot, i % per_slot - ups
         cols = pl.ds(pl.multiple_of(tile * 256, 256), 256)
-        return (pltpu.make_async_copy(down_hbm.at[slot, :, cols], w_v.at[i % bufs, pl.ds(0, ff), :], w_sem.at[i % bufs, 0]),)
+        return [pltpu.make_async_copy(down_hbm.at[slot, pl.ds(part * (ff // 2), ff // 2), cols],
+                                      w_v.at[i % bufs, pl.ds(part * (ff // 2), ff // 2), :], w_sem.at[i % bufs, part]) for part in (0, 1)]
 
     def fetch(i):
-        @pl.when(i % per_slot < ups)
-        def _():
-            for copy in up_copies(i):
-                copy.start()
+        @pl.when((i % per_slot < whole) & (i % per_slot % 2 == 0))
+        def _():
+            wide_copy(i, gate_hbm).start()
+
+        @pl.when((i % per_slot < whole) & (i % per_slot % 2 == 1))
+        def _():
+            wide_copy(i, up_hbm).start()
+
+        if whole < ups:
+            @pl.when(i % per_slot == whole)
+            def _():
+                for copy in pair_copies(i):
+                    copy.start()
 
         @pl.when(i % per_slot >= ups)
         def _():
@@ -66,13 +82,25 @@
     def one(i, _):
         slot, k, buf = i // per_slot, i % per_slot, i % bufs
 
-        @pl.when(k < ups)
-        def _():
-            for copy in up_copies(i):
-                copy.wait()
-            both = jnp.dot(rows_v[slot], w_v[buf], preferred_element_type=jnp.float32)
-            cols = pl.ds(pl.multiple_of(k * 128, 128), 128)
-            h_v[:rows, cols] = (jax.nn.silu(both[:, :128]) * both[:, 128:]).astype(jnp.bfloat16)
+        @pl.when((k < whole) & (k % 2 == 0))
+        def _():
+            wide_copy(i, gate_hbm).wait()
+            g_v[...] = jnp.dot(rows_v[slot], w_v[buf], preferred_element_type=jnp.float32)
+
+        @pl.when((k < whole) & (k % 2 == 1))
+        def _():
+            wide_copy(i, up_hbm).wait()
+            up_act = jnp.dot(rows_v[slot], w_v[buf], preferred_element_type=jnp.float32)
+            cols = pl.ds(pl.multiple_of(k // 2 * 256, 256), 256)
+            h_v[:rows, cols] = (jax.nn.silu(g_v[...]) * up_act).astype(jnp.bfloat16)
+
+        if whole < ups:
+            @pl.when(k == whole)
+            def _():
+                for copy in pair_copies(i):
+                    copy.wait()
+                both = jnp.dot(rows_v[slot], w_v[buf], preferred_element_type=jnp.float32)
+                h_v[:rows, whole * 128:] = (jax.nn.silu(both[:, :128]) * both[:, 128:]).astype(jnp.bfloat16)
 
         @pl.when(k >= ups)
         def _():
@@ -107,7 +135,7 @@
 
 
 def gather_kernel(tok_hbm, meta_hbm, gate_hbm, up_hbm, down_hbm, shg_hbm, shu_hbm, shd_hbm, y_hbm, far_hbm, all_meta_hbm, z_hbm,
-                  tok_v, meta_v, rows_v, far_v, w_v, h_v, y_v, z_v,
+                  tok_v, meta_v, rows_v, far_v, w_v, g_v, h_v, y_v, z_v,
                   tok_sem, own_sem, w_sem, y_sem, far_sem, z_sem, keep_sem, send_sem, recv_sem, msend_sem, mrecv_sem):
     ring, _, sub_rows, hidden = tok_v.shape
     dev_slots = rows_v.shape[0]
@@ -257,7 +285,7 @@
         far_copy(place).start()
 
     open_slots, run_slots, close_slots, segs = slot_stream(
-        gate_hbm, up_hbm, down_hbm, rows_v, w_v, h_v.at[0], y_v, y_hbm, w_sem, y_sem)
+        gate_hbm, up_hbm, down_hbm, rows_v, w_v, g_v, h_v.at[0], y_v, y_hbm, w_sem, y_sem)
 
     open_stream(shared_copies)
     own_meta.wait()
@@ -347,6 +375,7 @@
             pltpu.VMEM((dev_slots, near * slot_cap, hidden), jnp.bfloat16),
             pltpu.VMEM((2, dev_slots, slot_cap, hidden), jnp.bfloat16),
             pltpu.VMEM((4, hidden, 256), jnp.bfloat16),
+            pltpu.VMEM((near * slot_cap, 256), jnp.float32),
             pltpu.VMEM((2, near * slot_cap, ff), jnp.bfloat16),
             pltpu.VMEM((2, near, slot_cap, 256), jnp.bfloat16),
             pltpu.VMEM((2, tok_count, 256), jnp.float32),
@@ -359,9 +388,9 @@
     )(tok_rows, meta, w_gate, w_up, w_down, sh_gate, sh_up, sh_down)
 
 
-def reduce_kernel(near_hbm, x_hbm, meta_hbm, gate_hbm, up_hbm, down_hbm, out_hbm, far_hbm,
-                  x_v, w_v, h_v, y_v, meta_v, weigh_v, tri_v, own_v, run_v,
-                  x_sem, w_sem, y_sem, tri_sem, meta_sem, send_sem, recv_sem, free_sem, out_sem):
+def reduce_kernel(near_hbm, x_hbm, meta_hbm, z_hbm, gate_hbm, up_hbm, down_hbm, out_hbm, far_hbm,
+                  z_v, x_v, w_v, g_v, h_v, y_v, meta_v, weigh_v, tri_v, own_v, run_v,
+                  z_sem, x_sem, w_sem, y_sem, tri_sem, meta_sem, send_sem, recv_sem, free_sem, out_sem):
     steps = meta_hbm.shape[0]
     near = near_hbm.shape[0]
     pair_rows = near_hbm.shape[1]
@@ -452,7 +481,7 @@
             device_id={'ep': ahead[way]}, device_id_type=MESH)
 
     open_slots, run_slots, close_slots, segs = slot_stream(
-        gate_hbm, up_hbm, down_hbm, x_v, w_v, h_v, y_v, far_hbm, w_sem, y_sem)
+        gate_hbm, up_hbm, down_hbm, x_v, w_v, g_v, h_v, y_v, far_hbm, w_sem, y_sem)
     per_step = -(-segs // (2 * early))
 
     for par in (0, 1):
@@ -524,15 +553,20 @@
             start_fetch(step + 3, False)
         return 0
 
+    z_copy = pltpu.make_async_copy(z_hbm, z_v, z_sem)
+    z_copy.start()
     lax.fori_loop(early, steps - 1, late_step, 0)
+    z_copy.wait()
     last = (steps - 1) % 2
     outs = []
     for sub in (0, 1):
         for way in (0, 1):
             send(steps - 2, way, sub).wait_recv()
             send(steps - 2, way, sub).wait_send()
-            run_v[way, last, sub] += own_v[way, sub * sub_rows:(sub + 1) * sub_rows, :]
-            outs.append(pltpu.make_async_copy(run_v.at[way, last, sub],
+            toks = slice(sub * sub_rows, (sub + 1) * sub_rows)
+            total = z_v[toks, way * half:(way + 1) * half] + (run_v[way, last, sub] + own_v[way, toks, :])
+            tri_v[1 - last, way, toks, :] = total.astype(jnp.bfloat16)
+            outs.append(pltpu.make_async_copy(tri_v.at[1 - last, way, pl.ds(sub * sub_rows, sub_rows), :],
                                               out_hbm.at[pl.ds(sub * sub_rows, sub_rows), pl.ds(way * half, half)],
                                               out_sem.at[way, sub]))
             outs[-1].start()
@@ -540,7 +574,7 @@
         copy.wait()
 
 
-def reduce_home(near_out, far_rows, meta, w_gate, w_up, w_down):
+def reduce_home(near_out, far_rows, meta, shared_out, w_gate, w_up, w_down):
     near, pair_rows, hidden = near_out.shape
     dev_slots, ff, _ = w_down.shape
     slot_cap = pair_rows // dev_slots
@@ -553,13 +587,15 @@
     flops = 6 * far * pair_rows * hidden * ff + 6 * steps * pair_rows * hidden * tok_count
     return pl.pallas_call(
         reduce_kernel,
-        out_shape=(jax.ShapeDtypeStruct((tok_count, hidden), jnp.float32),
+        out_shape=(jax.ShapeDtypeStruct((tok_count, hidden), jnp.bfloat16),
                    jax.ShapeDtypeStruct((far, pair_rows, hidden), jnp.bfloat16)),
-        in_specs=[any_spec] * 6,
+        in_specs=[any_spec] * 7,
         out_specs=(any_spec,) * 2,
         scratch_shapes=[
+            pltpu.VMEM((tok_count, hidden), jnp.float32),
             pltpu.VMEM((dev_slots, far * slot_cap, hidden), jnp.bfloat16),
             pltpu.VMEM((4, hidden, 256), jnp.bfloat16),
+            pltpu.VMEM((far * slot_cap, 256), jnp.float32),
             pltpu.VMEM((far * slot_cap, ff), jnp.bfloat16),
             pltpu.VMEM((2, far, slot_cap, 256), jnp.bfloat16),
             pltpu.VMEM((2, 2) + meta.shape[1:], jnp.float32),
@@ -567,13 +603,13 @@
             pltpu.VMEM((2, 2, 3 * wide, half), jnp.bfloat16),
             pltpu.VMEM((2, tok_count, half), jnp.float32),
             pltpu.VMEM((2, 2, 2, sub_rows, half), jnp.float32),
-            dma, dma((4, 2)), dma((2,)), dma((2, 2, 3)), dma((2, 2)), dma((2, 2, 2)), dma((2, 2, 2)),
+            dma, dma, dma((4, 2)), dma((2,)), dma((2, 2, 3)), dma((2, 2)), dma((2, 2, 2)), dma((2, 2, 2)),
             pltpu.SemaphoreType.REGULAR((2, 2)), dma((2, 2)),
         ],
         compiler_params=pltpu.CompilerParams(collective_id=1, has_side_effects=True, vmem_limit_bytes=65_000_000),
         cost_estimate=pl.CostEstimate(flops=flops, bytes_accessed=170_000_000, transcendentals=0),
         name='reduce_home',
-    )(near_out, far_rows, meta, w_gate, w_up, w_down)[0]
+    )(near_out, far_rows, meta, shared_out, w_gate, w_up, w_down)[0]
 
 
 def solution(mesh):
@@ -597,8 +633,7 @@
         dest = slot_idx.astype(jnp.float32) * slot_cap + jnp.sum(jnp.where(match, rank[:, None, :], 0.0), axis=2)
         meta = jnp.concatenate([dest, gate_wts, jnp.zeros((tok_count, 16 - 2 * top_k), jnp.float32)], axis=1).T
         near_out, far_rows, all_meta, shared_out = gather_rows(tok_rows, meta, w_gate, w_up, w_down, sh_gate, sh_up, sh_down, ep_size, slot_cap)
-        routed = reduce_home(near_out, far_rows, all_meta, w_gate, w_up, w_down)
-        return (shared_out + routed).astype(jnp.bfloat16)
+        return reduce_home(near_out, far_rows, all_meta, shared_out, w_gate, w_up, w_down)
 
     tok_spec = P(('dp', 'ep'), None)
     slot_spec = P('ep', None, None)

time: 609 us -> 614 us (level)
  no operation moved by 1% of the time
where the time goes in v5:
time: 614 us; the launch traced here: 610 us
  Pallas kernels  600 us (98%)
    pallas_call x1, Pallas kernels, reduce_home(): pl.pallas_call(reduce_kernel, out_shape=(jax.ShapeDtypeStruct((tok_count,...  387 us
    pallas_call x1, Pallas kernels, gather_rows(): pl.pallas_call(gather_kernel, out_shape=(jax.ShapeDtypeStruct((near, dev_...  213 us

profile of v5, /device:TPU:0, one launch (start us, length us, event | category | flops | bytes accessed | tf_op | source)
XLA Modules:
  0.0 610.1 jit_solution(14785318495272707654)
XLA Ops:
  0.0 0.1 pad.2.clone
  0.1 0.8 fusion.4
  0.9 0.3 fusion.3
  1.2 0.8 select_reduce_fusion.2
  2.0 2.4 fusion.2
  4.4 0.9 select_reduce_fusion
  5.3 0.7 divide_multiply_fusion
  6.0 0.7 maximum_bitcast_fusion.meta_hbm
  6.7 212.7 %gather_rows.1 = (bf16[9,400,2048]{2,1,0:T(8,128)(2,1)}, bf16[5,560,2048]{2,1,0:T(8,128)(2,1)}, f32[16,16,512]{2,1,0:T(8,128)}, f32[512,2048]{1,0:T(8,128)}) custom-call(bf16[512,2048]{1,0:T(8,128)(2,1)} %tok_hbm.1, f32[16,512]{1,0:T(8,128)} %maximum_bitcast_fusion.meta_hbm, bf16[5,2048,1408]{2,1,0:T(8,128)(2,1)} %gate_hbm.3, bf16[5,2048,1408]{2,1,0:T(8,128)(2,1)} %up_hbm.3, ...), custom_call_target="tpu_custom_call" | custom-call | flops 80002154496 | bytes 170000000 | tf_op jit(solution)/shard_map/gather_rows/pallas_call | solution.py:364
  219.5 387.4 %reduce_home.1 = (bf16[512,2048]{1,0:T(8,128)(2,1)}, bf16[7,400,2048]{2,1,0:T(8,128)(2,1)}) custom-call(bf16[9,400,2048]{2,1,0:T(8,128)(2,1)} %get-tuple-element.10.near_hbm, bf16[5,560,2048]{2,1,0:T(8,128)(2,1)} %get-tuple-element.11.x_hbm, f32[16,16,512]{2,1,0:T(8,128)} %get-tuple-element.12.meta_hbm, f32[512,2048]{1,0:T(8,128)} %get-tuple-element.13.z_hbm, ...), custom_call_target="tpu_custom_call" | custom-call | flops 88709529600 | bytes 170000000 | tf_op jit(solution)/shard_map/reduce_home/pallas_call | solution.py:588
  606.9 3.2 copy.16
  (1 shorter events, 0.0 us)
